TPU v7x, 256 devices: a whole 4x4x8 slice. The times are simulated.
256 devices in a mesh: segment: 8 (over y, core), shard: 32 (over x, z).
Axes of the slice: x: 4, y: 4, z: 8, core: 2. Of those that a mesh axis runs over, the one named last changes fastest.
Arguments:
- buffer: bfloat16 [16, 18432, 2304], P('segment', 'shard'), may hold values from -6 to 6
- right_basis: bfloat16 [16, 2304, 256], P('segment', 'shard'), may hold values from -0.125 to 0.125
- layer_count: int32 [8], P('segment'), may hold values from 1 to 2, as said below
Outputs:
- momentum_out: bfloat16 [16, 18432, 2304], P('segment', 'shard')
- left_step: bfloat16 [16, 18432, 256], P('segment', 'shard')
- right_step: float32 [16, 2304, 256], P('segment', 'shard')
Inputs may be any that keep to these rules, and one draw needn't show every extreme that they name: `layer_count`: each segment uses between 1 and 2 slots; some segment uses 2 and some segment uses 1.
All inputs are finite; a program needn't handle non-finite values.
Results may differ from a plain program's by a relative error of at most 0.0024.
Values may be sent and summed in bfloat16 or wider, within the bound.
No kernel may reach another device: no remote copies, remote signals or barrier semaphores. Data moves between devices by JAX's collectives and lax.ppermute only.
A program may use at most 64 MiB of HBM per device.

v0:
```python
import math

import jax
import jax.numpy as jnp
from jax import lax
from jax.sharding import Mesh
from jax.sharding import PartitionSpec as P

SHARD = ("shard_0", "shard_1")
SEGMENT = ("segment_0", "segment_1")


MOMENTUM = 0.9
CLIP_RMS = 0.35
SQUARE_FLOOR = 0.0625


def sent_to_all(shard, axis):
    copies = jnp.broadcast_to(shard, (lax.axis_size(axis), *shard.shape))
    return lax.all_to_all(copies, axis, split_axis=0, concat_axis=0, tiled=True)


def over_copies(shard, axis):
    return sent_to_all(shard, axis).sum(axis=0)


def over_axes(shard, axes):
    far, near = axes
    return over_copies(over_copies(shard, near), far)


def together(arrays, axis):
    ends = [0]
    for a in arrays:
        ends.append(ends[-1] + a.size)
    running = over_axes(jnp.concatenate([a.ravel() for a in arrays]), axis)
    return tuple((running[b:e].reshape(a.shape) for a, b, e in zip(arrays, ends, ends[1:])))


def joined_along(blocks, dim):
    shape = list(blocks.shape[1:])
    shape[dim] *= blocks.shape[0]
    return jnp.moveaxis(blocks, 0, dim).reshape(shape)


def stacked_from(shard, axes, order):
    blocks = shard[None]
    for k in order:
        blocks = lax.all_gather(blocks, axes[k], axis=0, tiled=True)
    block = [lax.axis_size(axes[k]) for k in reversed(order)]
    blocks = blocks.reshape(*block, *shard.shape)
    turned = sorted(range(len(order)), key=lambda place: order[len(order) - 1 - place])
    return blocks.transpose(*turned, *range(len(order), blocks.ndim)).reshape(-1, *shard.shape)


def whole_of(shard, axes, order, dim):
    return joined_along(stacked_from(shard, axes, order), dim)


def padded_to(lines, devices):
    spare = -len(lines) % devices
    return jnp.pad(lines, [(0, spare)] + [(0, 0)] * (lines.ndim - 1))


def collect(shard, axis, dim):
    blocks = sent_to_all(shard, axis)
    return joined_along(blocks, dim)


def in_blocks(shard, dim, devices):
    before, after = (shard.shape[:dim], shard.shape[dim + 1 :])
    return jnp.moveaxis(shard.reshape(*before, devices, -1, *after), dim, 0)


def sent_and_summed(shard, axis, dim):
    blocks = in_blocks(shard, dim, lax.axis_size(axis))
    arrived = lax.all_to_all(blocks, axis, split_axis=0, concat_axis=0, tiled=True)
    return arrived.sum(axis=0)


def sum_by_parts(shard, axes):
    lines = shard.reshape(-1, shard.shape[-1])
    padded = padded_to(lines, lax.axis_size(axes))
    whole = collect(sent_and_summed(padded, axes, 0), axes, 0)
    return lax.slice_in_dim(whole, 0, len(lines)).reshape(shard.shape)


def finish_basis(proj, gram):
    lower = jnp.linalg.cholesky(gram)
    solved = jax.scipy.linalg.solve_triangular(lower, jnp.swapaxes(proj, 1, 2), lower=True)
    return jnp.swapaxes(solved, 1, 2)


def right_factor(partial_value):
    groups = lax.axis_size(SHARD)
    cols = partial_value.shape[1]
    width = cols // groups
    full = lax.psum(partial_value, SHARD)
    colsq = jnp.sum(full * full, axis=1, keepdims=True)
    scaled = full * (math.sqrt(cols) * lax.rsqrt(colsq + 1.0))
    local = lax.dynamic_slice_in_dim(scaled, lax.axis_index(SHARD) * width, width, 1)
    return (full.astype(jnp.bfloat16), local)


def finish_layers(block, proj, gram, used, clip, rows_all):
    ortho = finish_basis(proj, gram)
    half_left = ortho.astype(jnp.bfloat16)
    partial_value = jnp.einsum("kij,kir->kjr", block, half_left, preferred_element_type=jnp.float32)
    half_right, right_local = right_factor(partial_value)
    correction = jnp.einsum(
        "kir,kjr->kij", half_left, half_right, preferred_element_type=jnp.float32
    )
    keep = used[:, None, None]
    moment = jnp.where(keep, block - (1.0 - MOMENTUM) * correction, 0.0).astype(jnp.bfloat16)
    left = jnp.where(keep, clip * math.sqrt(rows_all) * ortho, 0.0).astype(jnp.bfloat16)
    right = jnp.where(keep, right_local, 0.0)
    return (moment, left, right)


def body(buffer, right_basis, layer_count):
    slots = buffer.shape[0]
    rows_dev = buffer.shape[1]
    cols = buffer.shape[2]
    rows_all = rows_dev * lax.axis_size(SHARD)
    count = layer_count[0]
    used = jnp.arange(slots, dtype=jnp.int32) < count
    per_slot = jnp.sum(jnp.square(buffer.astype(jnp.float32)), axis=(1, 2))
    local_sq = jnp.sum(jnp.where(used, per_slot, 0.0))
    local_elems = count.astype(jnp.float32) * float(rows_dev * cols)
    total_sq, total_elems = together(
        (local_sq, local_elems), (("segment_0", "segment_1"), ("shard_0", "shard_1"))
    )
    clip = jnp.minimum(1.0, CLIP_RMS * lax.rsqrt(jnp.maximum(total_sq / total_elems, SQUARE_FLOOR)))
    proj = jnp.einsum(
        "kij,kjr->kir",
        buffer,
        whole_of(right_basis, SHARD, (0, 1), 1),
        preferred_element_type=jnp.float32,
    )
    local_gram = jnp.einsum("kir,kis->krs", proj, proj, precision=lax.Precision.HIGHEST)
    gram = sum_by_parts(local_gram, SHARD)
    return finish_layers(buffer, proj, gram, used, clip, rows_all)


def solution(mesh):
    split = Mesh(mesh.devices.reshape(4, 2, 4, 8), ("segment_0", "segment_1", "shard_0", "shard_1"))
    in_specs = (P(SEGMENT, SHARD, None), P(SEGMENT, SHARD, None), P(SEGMENT))
    out_specs = (P(SEGMENT, SHARD, None), P(SEGMENT, SHARD, None), P(SEGMENT, SHARD, None))
    return jax.shard_map(body, mesh=split, in_specs=in_specs, out_specs=out_specs, check_vma=False)
```

profile of v0, /device:TPU:24, one launch (start us, length us, event | category | flops | bytes accessed | tf_op | source)
XLA Modules:
  0.0 417.4 jit_solution(7943866810444784080)
XLA Ops:
  7.2 0.0 all-gather.3.cloned.1.call-start
  7.2 14.3 %all-gather = bf16[8,72,256]{2,1,0:T(8,128)(2,1)} all-gather(bf16[2,72,256]{2,1,0:T(8,128)(2,1)} %param.4), channel_id=2, replica_groups=mesh['segment_0'=4,'segment_1'=2,'shard_0'=4,'shard_1'=8] {'shard_0'}, dimensions={0}, use_global_device_ids=true | all-gather | bytes 368640 | tf_op jit(solution)/shard_map/all_gather | solution.py:49
  21.5 0.0 all-gather.3.cloned.1.call-update
  21.5 42.8 %all-gather.3.cloned.1.call-done = bf16[32,2,72,256]{3,2,1,0:T(8,128)(2,1)} async-done(((bf16[4,2,72,256]{3,2,1,0:T(8,128)(2,1)}), bf16[32,2,72,256]{3,2,1,0:T(8,128)(2,1)}) %all-gather.3.cloned.1.call-update) | async-done | bytes 2359312 | tf_op jit(solution)/shard_map/all_gather | solution.py:49
  64.3 1.8 copy.42
  66.1 4.0 fusion.21
  70.2 2.3 fusion.22
  72.5 21.7 %all_to_all.22 = f32[32,16,256]{2,1,0:T(8,128)S(1)} all-to-all(f32[32,16,256]{2,1,0:T(8,128)S(1)} %bitcast.72), channel_id=1, replica_groups=mesh['segment_0'=4,'segment_1'=2,'shard_0'=4,'shard_1'=8] {'shard_0','sh..., dimensions={0} | all-to-all | bytes 1048576 | tf_op jit(solution)/shard_map/all_to_all | solution.py:77
  94.3 0.9 broadcast_in_dim.60
  95.1 4.1 all-to-all-start.1
  99.2 0.2 all-reduce.3.cloned.1.call-start
  99.5 13.5 %all-to-all-done.1 = f32[32,16,256]{2,1,0:T(8,128)S(1)} async-done(((f32[32,16,256]{2,1,0:T(8,128)}), f32[32,16,256]{2,1,0:T(8,128)S(1)}, u32[]{:S(2)}, u32[]{:S(2)}) %all-to-all-start.1) | async-done | bytes 524320 | tf_op jit(solution)/shard_map/all_to_all | solution.py:20
  113.0 0.2 copy.43
  113.2 0.1 fusion.8
  113.3 23.5 %custom-call.17 = f32[2,128,128]{2,1,0:T(8,128)S(1)} custom-call(f32[2,128,128]{2,1,0:T(8,128)S(1)} %cholesky.122), custom_call_target="Cholesky" | custom-call | tf_op jit(solution)/shard_map/jit(cholesky)/cholesky | solution.py:89
  136.8 19.7 %custom-call.18 = f32[2,1,128,128]{2,3,1,0:T(8,128)S(1)} custom-call(f32[2,1,128,128]{3,2,1,0:T(8,128)S(1)} %select_bitcast_fusion), custom_call_target="InvertDiagBlocksLowerTriangular" | custom-call | tf_op jit(solution)/shard_map/jit(cholesky)/cholesky | solution.py:89
  156.5 0.3 constant_dynamic-update-slice_fusion.1
  156.8 0.4 convolution_subtract_fusion.1
  157.2 23.5 %custom-call.19 = f32[2,128,128]{2,1,0:T(8,128)S(1)} custom-call(f32[2,128,128]{2,1,0:T(8,128)S(1)} %convolution_subtract_fusion.1), custom_call_target="Cholesky" | custom-call | tf_op jit(solution)/shard_map/jit(cholesky)/cholesky | solution.py:89
  180.7 0.2 compare_reduce_fusion
  180.8 0.1 select_select_fusion
  181.0 0.1 triangular_solve.62
  181.1 4.0 while.1
  181.1 0.6 fusion.33
  181.7 1.4 bitcast_dynamic-update-slice_fusion.2
  183.1 0.6 fusion.33
  183.7 1.4 bitcast_dynamic-update-slice_fusion.2
  185.1 39.5 %custom-call.20 = f32[2,2,128,128]{2,3,1,0:T(8,128)S(1)} custom-call(f32[2,2,128,128]{3,2,1,0:T(8,128)S(1)} %bitcast.74), custom_call_target="InvertDiagBlocksLowerTriangular" | custom-call | tf_op jit(solution)/shard_map/jit(_solve_triangular)/vmap()/triangular_solve | solution.py:90
  224.6 0.6 fusion.6
  225.3 0.6 convolution_subtract_fusion
  225.9 0.6 fusion.11
  226.6 6.7 %convolution_bitcast_fusion = f32[2,2304,256]{1,2,0:T(8,128)} fusion(bf16[2,576,2304]{2,1,0:T(8,128)(2,1)} %param.3, f32[2,128,576]{1,2,0:T(8,128)S(1)} %fusion.11, f32[2,128,576]{1,2,0:T(8,128)S(1)} %fusion.6), kind=kOutput, calls=%fused_computation.7 | convolution fusion | flops 1360134144 | bytes 11206656 | tf_op jit(solution)/shard_map/kij,kir->kjr/dot_general | solution.py:108
  233.3 0.0 all-reduce.3.cloned.1.call-update
  234.0 4.0 fusion.2
  238.0 0.6 select_reduce_fusion.2
  238.6 0.6 pad_maximum_fusion.1
  239.2 0.6 broadcast_in_dim.64
  239.8 4.6 %all-to-all-start.2 = ((f32[32,1,2]{2,1,0:T(1,128)}), f32[32,1,2]{2,1,0:T(1,128)S(1)}, u32[]{:S(2)}, u32[]{:S(2)}) async-start(f32[32,1,2]{2,1,0:T(1,128)} %broadcast_in_dim.64), calls=%async_computation.2 | async-start | bytes 32768 | tf_op jit(solution)/shard_map/all_to_all | solution.py:20
  244.4 9.9 %all-to-all-done.2 = f32[32,1,2]{2,1,0:T(1,128)S(1)} async-done(((f32[32,1,2]{2,1,0:T(1,128)}), f32[32,1,2]{2,1,0:T(1,128)S(1)}, u32[]{:S(2)}, u32[]{:S(2)}) %all-to-all-start.2) | async-done | bytes 288 | tf_op jit(solution)/shard_map/all_to_all | solution.py:20
  254.3 0.1 reduce_sum.57
  254.4 0.6 broadcast_in_dim.65
  255.0 4.8 %all-to-all-start.3 = ((f32[8,1,2]{2,1,0:T(1,128)}), f32[8,1,2]{2,1,0:T(1,128)S(1)}, u32[]{:S(2)}, u32[]{:S(2)}) async-start(f32[8,1,2]{2,1,0:T(1,128)} %broadcast_in_dim.65), calls=%async_computation.3 | async-start | bytes 8192 | tf_op jit(solution)/shard_map/all_to_all | solution.py:20
  259.8 3.1 all-to-all-done.3
  263.0 0.6 fusion.20
  264.9 1.0 fusion.5
  266.0 131.5 %all-reduce.3.cloned.1.call-done = f32[2,2304,256]{1,2,0:T(8,128)} async-done(((f32[2,2304,256]{1,2,0:T(8,128)}), f32[2,2304,256]{1,2,0:T(8,128)}) %all-reduce.3.cloned.1.call-update) | async-done | bytes 4718608 | tf_op jit(solution)/shard_map/psum | solution.py:98
  397.5 2.7 multiply_reduce_fusion
  400.2 1.3 fusion.9
  401.5 0.8 copy.52
  402.3 8.3 %fusion.1 = bf16[2,576,2304]{2,1,0:T(8,128)(2,1)} fusion(bf16[2,576,2304]{2,1,0:T(8,128)(2,1)} %param.3, pred[2]{0:T(512)(128)(4,1)S(1)} %iota_compare_fusion.3, f32[2,2304,256]{1,2,0:T(8,128)} %all-reduce.3.cloned.1.call-done, f32[2,128,576]{1,2,0:T(8,128)S(1)} %fusion.11, f32[2,128,576]{1,2,0:T(8,128)S(1)} %fusion.6), kind=kOutput, calls=%fused_computation.5 | convolution fusion | flops 1374584832 | bytes 16515074 | tf_op jit(solution)/shard_map/kir,kjr->kij/dot_general | solution.py:110
  (16 shorter events, 0.3 us)
Async XLA Ops:
  7.2 57.1 %all-gather.3.cloned.1.call-start = ((), (), s32[]{:S(2)}) async-start(), calls=%async_computation.4 | async-start | bytes 2654208 | tf_op jit(solution)/shard_map/all_gather | solution.py:49
  95.1 17.9 %all-to-all-start.1 = ((f32[32,16,256]{2,1,0:T(8,128)}), f32[32,16,256]{2,1,0:T(8,128)S(1)}, u32[]{:S(2)}, u32[]{:S(2)}) async-start(f32[32,16,256]{2,1,0:T(8,128)} %broadcast_in_dim.60), calls=%async_computation.1 | async-start | bytes 1048576 | tf_op jit(solution)/shard_map/all_to_all | solution.py:20
  99.2 298.3 %all-reduce.3.cloned.1.call-start = ((), (), s32[]{:S(2)}) async-start(), calls=%async_computation.5 | async-start | bytes 9437184 | tf_op jit(solution)/shard_map/psum | solution.py:98
  239.8 14.5 %all-to-all-start.2 = ((f32[32,1,2]{2,1,0:T(1,128)}), f32[32,1,2]{2,1,0:T(1,128)S(1)}, u32[]{:S(2)}, u32[]{:S(2)}) async-start(f32[32,1,2]{2,1,0:T(1,128)} %broadcast_in_dim.64), calls=%async_computation.2 | async-start | bytes 32768 | tf_op jit(solution)/shard_map/all_to_all | solution.py:20
  255.0 7.9 %all-to-all-start.3 = ((f32[8,1,2]{2,1,0:T(1,128)}), f32[8,1,2]{2,1,0:T(1,128)S(1)}, u32[]{:S(2)}, u32[]{:S(2)}) async-start(f32[8,1,2]{2,1,0:T(1,128)} %broadcast_in_dim.65), calls=%async_computation.3 | async-start | bytes 8192 | tf_op jit(solution)/shard_map/all_to_all | solution.py:20
Sparse Core Ops, SparseCore 0:
  21.6 42.6 all-gather.2
  233.5 163.9 all-reduce.2
where the time goes:
time: 418 us; the launch traced here: 417 us
  waiting for transfers between devices  201 us (48%)
  other arithmetic  117 us (28%)
  blocking collectives  36 us (9%)
  matrix products  24 us (6%)
  between operations  16.3 us (4%)
  starting transfers between devices  13.7 us (3%)
  local copies, waits for them, and re-layouts  9.55 us (2%)
    psum x1, waiting for transfers between devices, right_factor(): full = lax.psum(partial_value, SHARD)  132 us
    another operation x9, other arithmetic, finish_basis(): lower = jnp.linalg.cholesky(gram)  66.8 us
    all_gather x1, waiting for transfers between devices, stacked_from(): blocks = lax.all_gather(blocks, axes[k], axis=0, tiled=True)  42.8 us
    another operation x4, other arithmetic, finish_basis(): jax.scipy.linalg.solve_triangular(lower, jnp.swapaxes(proj, 1, 2), lower=...  39.7 us
    all_to_all x3, waiting for transfers between devices, sent_to_all(): return lax.all_to_all(copies, axis, split_axis=0, concat_axis=0, tiled=True)  26.5 us
    all_to_all x1, blocking collectives, sent_and_summed(): lax.all_to_all(blocks, axis, split_axis=0, concat_axis=0, tiled=True)  21.7 us
    all_gather x1, blocking collectives, stacked_from(): blocks = lax.all_gather(blocks, axes[k], axis=0, tiled=True)  14.3 us
    all_to_all x3, starting transfers between devices, sent_to_all(): return lax.all_to_all(copies, axis, split_axis=0, concat_axis=0, tiled=True)  13.5 us
  transfers between devices with their start and end apart: 5, of which 5 were waited for; matrix products, arithmetic and copies ran while one was open for 2% of the time, Pallas kernels for 0%

commit v1 on v0

v1 whole, which is shorter than its diff:
```python
import math

import jax
import jax.numpy as jnp
from jax import lax
from jax.experimental import pallas as pl
from jax.experimental.pallas import tpu as pltpu
from jax.sharding import Mesh
from jax.sharding import PartitionSpec as P

SEG = ("segment_0", "segment_1")
X = "shard_0"
Z = "shard_1"
SHARD = (X, Z)

MOMENTUM = 0.9
CLIP_RMS = 0.35
SQUARE_FLOOR = 0.0625
BLOCK = 16
F32 = jnp.float32
BF16 = jnp.bfloat16


def exchange(blocks, axis):
    return lax.all_to_all(blocks, axis, split_axis=0, concat_axis=0, tiled=True)


def spread(value, axis):
    return exchange(jnp.broadcast_to(value, (lax.axis_size(axis), *value.shape)), axis)


def whole_rows(shard):
    slots, rows, rank = shard.shape
    line = spread(shard, Z)
    plane = spread(line, X)
    return plane.reshape(-1, slots, rows, rank).transpose(1, 0, 2, 3).reshape(slots, -1, rank)


def inverse_factor_kernel(gram_ref, out_ref, work_ref):
    slots, n, _ = gram_ref.shape
    b = BLOCK
    for s in range(slots):
        row = lax.broadcasted_iota(jnp.int32, (n, n), 0)
        col = lax.broadcasted_iota(jnp.int32, (n, n), 1)
        work_ref[s, :, :n] = gram_ref[s]
        work_ref[s, :, n:] = (row == col).astype(F32)
    sub = lax.broadcasted_iota(jnp.int32, (b, 128), 0)
    for j in range(n // b):
        lo, hi = j * b, (j + 1) * b
        panels = []
        cols = []
        for s in range(slots):
            panel = work_ref[s, lo:hi, :]
            panels.append(panel)
            cols.append([jnp.broadcast_to(panel[:, lo + k : lo + k + 1], (b, 128)) for k in range(b)])
        for k in range(b):
            for s in range(slots):
                c = cols[s]
                inv = lax.rsqrt(jnp.broadcast_to(c[k][k : k + 1], (b, 128)))
                scaled = c[k] * inv
                below = jnp.where(sub > k, scaled, 0.0)
                for i in range(k + 1, b):
                    c[i] = c[i] - below * jnp.broadcast_to(scaled[i : i + 1], (b, 128))
                p = panels[s]
                inv_row = jnp.concatenate([inv[:1]] * (2 * n // 128), axis=1)
                pivot = p[k : k + 1] * inv_row
                below_all = jnp.concatenate([below] * (2 * n // 128), axis=1)
                at_k = jnp.concatenate([sub == k] * (2 * n // 128), axis=1)
                pivot_all = jnp.broadcast_to(pivot, (b, 2 * n))
                panels[s] = jnp.where(at_k, pivot_all, p - below_all * pivot_all)
        for s in range(slots):
            work_ref[s, lo:hi, :] = panels[s]
            if hi < n:
                tail = panels[s][:, hi:n]
                update = lax.dot_general(
                    tail, panels[s], (((0,), (0,)), ((), ())),
                    precision=lax.Precision.HIGHEST, preferred_element_type=F32,
                )
                work_ref[s, hi:, :] = work_ref[s, hi:, :] - update
    for s in range(slots):
        out_ref[s] = work_ref[s, :, n:]


def inverse_factor(gram):
    slots, n, _ = gram.shape
    return pl.pallas_call(
        inverse_factor_kernel,
        out_shape=jax.ShapeDtypeStruct(gram.shape, F32),
        scratch_shapes=[pltpu.VMEM((slots, n, 2 * n), F32)],
        in_specs=[pl.BlockSpec(memory_space=pltpu.VMEM)],
        out_specs=pl.BlockSpec(memory_space=pltpu.VMEM),
        compiler_params=pltpu.CompilerParams(vmem_limit_bytes=16 << 20),
        name="inverse_factor",
    )(gram)


def body(buffer, right_basis, layer_count):
    slots, rows_dev, cols = buffer.shape
    rank = right_basis.shape[-1]
    devices = lax.axis_size(SHARD)
    near, far = lax.axis_size(Z), lax.axis_size(X)
    rows_all = rows_dev * devices
    width = cols // devices
    count = layer_count[0]
    used = jnp.arange(slots, dtype=jnp.int32) < count
    keep = used[:, None, None]

    basis = whole_rows(right_basis)
    proj = jnp.einsum("kij,kjr->kir", buffer, basis, preferred_element_type=F32)
    gram = jnp.einsum("kir,kis->krs", proj, proj, precision=lax.Precision.HIGHEST)
    per_slot = jnp.sum(jnp.square(buffer.astype(F32)), axis=(1, 2))
    row = lax.broadcasted_iota(jnp.int32, gram.shape, 1)
    col = lax.broadcasted_iota(jnp.int32, gram.shape, 2)
    gram = jnp.where((row == 0) & (col == rank - 1), per_slot[:, None, None], gram)
    part = exchange(gram.reshape(devices, -1, rank), SHARD).sum(axis=0)
    gram = spread(part, SHARD).reshape(slots, rank, rank)
    squares = jnp.sum(jnp.where(used, gram[:, 0, rank - 1], 0.0))
    elements = count.astype(F32) * float(rows_all * cols)
    gram = jnp.where((row == 0) & (col == rank - 1), gram[:, rank - 1 :, :1], gram)

    lane = lax.broadcasted_iota(jnp.int32, (8, 128), 1)
    both = jnp.where(lane == 0, squares, elements)
    totals = spread(both, SEG)[:, 0, :2].sum(axis=0)
    clip = jnp.minimum(1.0, CLIP_RMS * lax.rsqrt(jnp.maximum(totals[0] / totals[1], SQUARE_FLOOR)))

    inverse = inverse_factor(gram)
    ortho = jnp.einsum("kir,ksr->kis", proj, inverse, precision=lax.Precision.HIGHEST)
    half_left = ortho.astype(BF16)
    left = jnp.where(keep, clip * math.sqrt(rows_all) * ortho, 0.0).astype(BF16)

    partial = jnp.einsum("kij,kir->kjr", buffer, half_left, preferred_element_type=F32)
    partial = partial.astype(BF16).reshape(slots, far, near * width, rank).transpose(1, 0, 2, 3)
    line = exchange(partial, X).astype(F32).sum(axis=0)
    line = line.reshape(slots, near, width, rank).transpose(1, 0, 2, 3)
    right = exchange(line, Z).sum(axis=0)
    half_right = whole_rows(right.astype(BF16))
    colsq = jnp.sum(jnp.square(half_right.astype(F32)), axis=1, keepdims=True)
    right_step = jnp.where(keep, right * (math.sqrt(cols) * lax.rsqrt(colsq + 1.0)), 0.0)

    correction = jnp.einsum("kir,kjr->kij", half_left, half_right, preferred_element_type=F32)
    moment = jnp.where(keep, buffer - (1.0 - MOMENTUM) * correction, 0.0).astype(BF16)
    return moment, left, right_step


def solution(mesh):
    split = Mesh(mesh.devices.reshape(4, 2, 4, 8), (*SEG, *SHARD))
    specs = (P(SEG, SHARD, None), P(SEG, SHARD, None), P(SEG))
    outs = (P(SEG, SHARD, None),) * 3
    return jax.shard_map(body, mesh=split, in_specs=specs, out_specs=outs, check_vma=False)
```

time: 418 us -> 266 us (0.64)
  waiting for transfers between devices: 201 us -> 37.7 us
  blocking collectives: 36 us -> 163 us
  other arithmetic: 117 us -> 7.34 us
  between operations: 16.3 us -> 2.86 us
  Pallas kernels: 0 us -> 12.5 us
  matrix products: 24 us -> 18.9 us
    all_to_all x1 -> x6, blocking collectives: 21.7 us -> 163 us  [exchange(): return lax.all_to_all(blocks, axis, split_axis=0, concat_axis=0, tiled=True)]
    psum x1 -> x0, waiting for transfers between devices: 132 us -> none  [right_factor(): full = lax.psum(partial_value, SHARD)]
    another operation x13 -> x0, other arithmetic: 107 us -> none  [the longest x9 66.8 us: finish_basis(): lower = jnp.linalg.cholesky(gram)]
    all_gather x1 -> x0, waiting for transfers between devices: 42.8 us -> none  [stacked_from(): blocks = lax.all_gather(blocks, axes[k], axis=0, tiled=True)]
    all_gather x1 -> x0, blocking collectives: 14.3 us -> none  [stacked_from(): blocks = lax.all_gather(blocks, axes[k], axis=0, tiled=True)]
    pallas_call x0 -> x1, Pallas kernels: none -> 12.5 us  [inverse_factor(): pl.pallas_call(inverse_factor_kernel, out_shape=jax.ShapeDtypeStruct(gram...]
    all_to_all x3, waiting for transfers between devices: 26.5 us -> 37.7 us  [exchange(): return lax.all_to_all(blocks, axis, split_axis=0, concat_axis=0, tiled=True)]
    another operation x10 -> x0, local copies, waits for them, and re-layouts: 4.29 us -> none
  transfers between devices with their start and end apart: 5 -> 3, of which waited for: 5 -> 2; matrix products, arithmetic and copies ran while one was open for 2% -> 2% of each run, Pallas kernels for 0% -> 5%
where the time goes in v1:
time: 266 us; the launch traced here: 265 us
  blocking collectives  163 us (61%)
  waiting for transfers between devices  37.7 us (14%)
  matrix products  18.9 us (7%)
  starting transfers between devices  14.5 us (5%)
  Pallas kernels  12.5 us (5%)
  local copies, waits for them, and re-layouts  8.78 us (3%)
  other arithmetic  7.34 us (3%)
  between operations  2.86 us (1%)
    all_to_all x6, blocking collectives, exchange(): return lax.all_to_all(blocks, axis, split_axis=0, concat_axis=0, tiled=True)  163 us
    all_to_all x3, waiting for transfers between devices, exchange(): return lax.all_to_all(blocks, axis, split_axis=0, concat_axis=0, tiled=True)  37.7 us
    all_to_all x3, starting transfers between devices, exchange(): return lax.all_to_all(blocks, axis, split_axis=0, concat_axis=0, tiled=True)  14.5 us
    pallas_call x1, Pallas kernels, inverse_factor(): pl.pallas_call(inverse_factor_kernel, out_shape=jax.ShapeDtypeStruct(gram...  12.5 us
    dot_general x1, matrix products, body(): jnp.einsum('kij,kir->kjr', buffer, half_left, preferred_element_type=F32)  6.2 us
  transfers between devices with their start and end apart: 3, of which 2 were waited for; matrix products, arithmetic and copies ran while one was open for 2% of the time, Pallas kernels for 5%

profile of v1, /device:TPU:24, one launch (start us, length us, event | category | flops | bytes accessed | tf_op | source)
XLA Modules:
  0.0 265.4 jit_solution(4922559733457072204)
XLA Ops:
  0.6 0.9 broadcast_in_dim.85
  1.6 27.2 %all_to_all.45 = bf16[8,2,72,256]{3,2,1,0:T(8,128)(2,1)S(1)} all-to-all(bf16[8,2,72,256]{3,2,1,0:T(8,128)(2,1)S(1)} %broadcast_in_dim.85), channel_id=1, replica_groups=mesh['segment_0'=4,'segment_1'=2,'shard_0'=4,'shard_1'=8] {'shard_1'}, dimensions={0} | all-to-all | bytes 1179648 | tf_op jit(solution)/shard_map/all_to_all | solution.py:25
  28.8 1.6 broadcast_in_dim.86
  30.3 4.3 %all-to-all-start.1 = ((bf16[4,8,2,72,256]{4,3,1,2,0:T(8,128)(2,1)}), bf16[4,8,2,72,256]{4,3,1,2,0:T(8,128)(2,1)S(1)}, u32[]{:S(2)}, u32[]{:S(2)}) async-start(bf16[4,8,2,72,256]{4,3,1,2,0:T(8,128)(2,1)} %broadcast_in_dim.86), calls=%async_computation.1 | async-start | bytes 4718592 | tf_op jit(solution)/shard_map/all_to_all | solution.py:25
  34.6 4.0 %fusion = f32[2]{0:T(128)S(1)} fusion(bf16[2,576,2304]{2,1,0:T(8,128)(2,1)} %param.3), kind=kLoop, calls=%fused_computation.2 | loop fusion | flops 7962622 | bytes 5308424 | tf_op jit(solution)/shard_map/reduce_sum | solution.py:111
  38.6 23.5 %all-to-all-done.1 = bf16[4,8,2,72,256]{4,3,1,2,0:T(8,128)(2,1)S(1)} async-done(((bf16[4,8,2,72,256]{4,3,1,2,0:T(8,128)(2,1)}), bf16[4,8,2,72,256]{4,3,1,2,0:T(8,128)(2,1)S(1)}, u32[]{:S(2)}, u32[]{:S(2)}) %all-to-all-start.1) | async-done | bytes 2359328 | tf_op jit(solution)/shard_map/all_to_all | solution.py:25
  62.1 0.2 copy.30
  62.3 0.2 copy.31
  62.5 4.0 %fusion.7 = f32[2,576,256]{2,1,0:T(8,128)S(1)} fusion(bf16[2,576,2304]{2,1,0:T(8,128)(2,1)} %param.3, bf16[2,2304,256]{2,1,0:T(8,128)(2,1)S(1)} %bitcast.43), kind=kOutput, calls=%fused_computation.25 | convolution fusion | flops 1358954496 | bytes 8847360 | tf_op jit(solution)/shard_map/kij,kjr->kir/dot_general | solution.py:109
  66.5 2.3 convolution_select_fusion
  68.8 19.6 %all_to_all.46 = f32[32,16,256]{2,1,0:T(8,128)S(1)} all-to-all(f32[32,16,256]{2,1,0:T(8,128)S(1)} %bitcast.46), channel_id=1, replica_groups=mesh['segment_0'=4,'segment_1'=2,'shard_0'=4,'shard_1'=8] {'shard_0','sh..., dimensions={0} | all-to-all | bytes 1048576 | tf_op jit(solution)/shard_map/all_to_all | solution.py:25
  88.5 0.9 broadcast_in_dim.88
  89.3 5.5 %all-to-all-start.3 = ((f32[32,16,256]{2,1,0:T(8,128)}), f32[32,16,256]{2,1,0:T(8,128)S(1)}, u32[]{:S(2)}, u32[]{:S(2)}) async-start(f32[32,16,256]{2,1,0:T(8,128)} %broadcast_in_dim.88), calls=%async_computation.3 | async-start | bytes 1048576 | tf_op jit(solution)/shard_map/all_to_all | solution.py:25
  95.5 14.1 %all-to-all-done.3 = f32[32,16,256]{2,1,0:T(8,128)S(1)} async-done(((f32[32,16,256]{2,1,0:T(8,128)}), f32[32,16,256]{2,1,0:T(8,128)S(1)}, u32[]{:S(2)}, u32[]{:S(2)}) %all-to-all-start.3) | async-done | bytes 524320 | tf_op jit(solution)/shard_map/all_to_all | solution.py:25
  109.6 0.2 slice_reduce_fusion.1
  109.8 0.6 select_reduce_fusion
  110.4 0.6 compare_select_fusion
  111.1 0.6 broadcast_in_dim.98
  111.7 4.7 %all-to-all-start.8 = ((f32[8,8,128]{2,1,0:T(8,128)}), f32[8,8,128]{2,1,0:T(8,128)S(1)}, u32[]{:S(2)}, u32[]{:S(2)}) async-start(f32[8,8,128]{2,1,0:T(8,128)} %broadcast_in_dim.98), calls=%async_computation.8 | async-start | bytes 65536 | tf_op jit(solution)/shard_map/all_to_all | solution.py:25
  116.4 0.2 and_select_fusion.gram_ref
  116.5 12.5 %inverse_factor.1 = f32[2,256,256]{2,1,0:T(8,128)S(1)} custom-call(f32[2,256,256]{2,1,0:T(8,128)S(1)} %and_select_fusion.gram_ref), custom_call_target="tpu_custom_call" | custom-call | tf_op jit(solution)/shard_map/inverse_factor/pallas_call | solution.py:86
  129.0 0.0 all-to-all-done.8
  129.1 0.6 fusion.6
  131.0 2.0 select_convert_fusion
  133.1 6.2 %fusion.3 = bf16[2,2304,256]{1,2,0:T(8,128)(2,1)} fusion(bf16[2,576,2304]{2,1,0:T(8,128)(2,1)} %param.3, bf16[2,576,256]{2,1,0:T(8,128)(2,1)S(1)} %get-tuple-element.8), kind=kOutput, calls=%fused_computation.8 | convolution fusion | flops 1360134144 | bytes 8257536 | tf_op jit(solution)/shard_map/kij,kir->kjr/dot_general | solution.py:131
  139.3 2.8 %copy.32 = bf16[2,2304,256]{2,1,0:T(8,128)(2,1)S(1)} copy(bf16[2,2304,256]{1,2,0:T(8,128)(2,1)} %fusion.3) | data formatting | bytes 4718592 | tf_op jit(solution)/shard_map/convert_element_type | solution.py:132
  142.1 0.2 copy.33
  142.3 32.3 %all_to_all.47 = bf16[4,2,576,256]{3,2,1,0:T(8,128)(2,1)S(1)} all-to-all(bf16[4,2,576,256]{3,2,1,0:T(8,128)(2,1)S(1)} %copy.33), channel_id=1, replica_groups=mesh['segment_0'=4,'segment_1'=2,'shard_0'=4,'shard_1'=8] {'shard_0'}, dimensions={0} | all-to-all | bytes 4718592 | tf_op jit(solution)/shard_map/all_to_all | solution.py:25
  174.6 0.3 convert_reduce_fusion
  175.0 0.1 copy.34
  175.1 35.2 %all_to_all.48 = f32[8,2,72,256]{3,2,1,0:T(8,128)S(1)} all-to-all(f32[8,2,72,256]{3,2,1,0:T(8,128)S(1)} %copy.34), channel_id=1, replica_groups=mesh['segment_0'=4,'segment_1'=2,'shard_0'=4,'shard_1'=8] {'shard_1'}, dimensions={0} | all-to-all | bytes 2359296 | tf_op jit(solution)/shard_map/all_to_all | solution.py:25
  210.3 0.1 reduce_sum.66
  210.4 19.8 %all_to_all.49 = bf16[8,2,72,256]{3,2,1,0:T(8,128)(2,1)S(1)} all-to-all(bf16[8,2,72,256]{3,2,1,0:T(8,128)(2,1)S(1)} %broadcast_in_dim.91), channel_id=1, replica_groups=mesh['segment_0'=4,'segment_1'=2,'shard_0'=4,'shard_1'=8] {'shard_1'}, dimensions={0} | all-to-all | bytes 1179648 | tf_op jit(solution)/shard_map/all_to_all | solution.py:25
  230.3 0.2 broadcast_in_dim.92
  230.5 0.0 slice-start
  230.5 28.8 %all_to_all.50 = bf16[4,8,2,72,256]{4,3,1,2,0:T(8,128)(2,1)S(1)} all-to-all(bf16[4,8,2,72,256]{4,3,1,2,0:T(8,128)(2,1)S(1)} %broadcast_in_dim.92), channel_id=1, replica_groups=mesh['segment_0'=4,'segment_1'=2,'shard_0'=4,'shard_1'=8] {'shard_0'}, dimensions={0} | all-to-all | bytes 4718592 | tf_op jit(solution)/shard_map/all_to_all | solution.py:25
  259.3 0.0 slice-start.1
  259.3 0.2 copy.36
  259.5 0.7 multiply_reduce_fusion
  260.2 0.7 multiply_select_fusion
  260.9 0.2 copy.37
  261.1 0.0 slice-done
  261.1 0.0 slice-done.1
  261.1 4.3 %fusion.2 = bf16[2,576,2304]{2,1,0:T(8,128)(2,1)} fusion(bf16[2,576,2304]{2,1,0:T(8,128)(2,1)S(1)} %bitcast.40, bf16[2,2304,256]{2,1,0:T(8,128)(2,1)S(1)} %bitcast.42, pred[2]{0:T(512)(128)(4,1)S(1)} %iota_compare_fusion.2, bf16[2,576,256]{2,1,0:T(8,128)(2,1)S(1)} %get-tuple-element.8), kind=kOutput, calls=%fused_computation.4 | convolution fusion | flops 1372225536 | bytes 13565954 | tf_op jit(solution)/shard_map/kir,kjr->kij/dot_general | solution.py:140
  (10 shorter events, 0.2 us)
Async XLA Ops:
  30.3 31.8 %all-to-all-start.1 = ((bf16[4,8,2,72,256]{4,3,1,2,0:T(8,128)(2,1)}), bf16[4,8,2,72,256]{4,3,1,2,0:T(8,128)(2,1)S(1)}, u32[]{:S(2)}, u32[]{:S(2)}) async-start(bf16[4,8,2,72,256]{4,3,1,2,0:T(8,128)(2,1)} %broadcast_in_dim.86), calls=%async_computation.1 | async-start | bytes 4718592 | tf_op jit(solution)/shard_map/all_to_all | solution.py:25
  89.3 20.3 %all-to-all-start.3 = ((f32[32,16,256]{2,1,0:T(8,128)}), f32[32,16,256]{2,1,0:T(8,128)S(1)}, u32[]{:S(2)}, u32[]{:S(2)}) async-start(f32[32,16,256]{2,1,0:T(8,128)} %broadcast_in_dim.88), calls=%async_computation.3 | async-start | bytes 1048576 | tf_op jit(solution)/shard_map/all_to_all | solution.py:25
  111.7 17.3 %all-to-all-start.8 = ((f32[8,8,128]{2,1,0:T(8,128)}), f32[8,8,128]{2,1,0:T(8,128)S(1)}, u32[]{:S(2)}, u32[]{:S(2)}) async-start(f32[8,8,128]{2,1,0:T(8,128)} %broadcast_in_dim.98), calls=%async_computation.8 | async-start | bytes 65536 | tf_op jit(solution)/shard_map/all_to_all | solution.py:25
  230.5 30.6 %slice-start = ((s8[5308416]{0:T(1024)(128)(4,1)}), s8[4194304]{0:T(1024)(128)(4,1)S(1)}, s32[]{:S(2)}) async-start(s8[5308416]{0:T(1024)(128)(4,1)} %bitcast.39), calls=%async_computation.9 | async-start | bytes 8388608
  259.3 1.8 slice-start.1

commit v2 on v1

--- a/solution.py
+++ b/solution.py
@@ -9,9 +9,11 @@
 from jax.sharding import PartitionSpec as P
 
 SEG = ("segment_0", "segment_1")
-X = "shard_0"
-Z = "shard_1"
-SHARD = (X, Z)
+X = "x"
+FAR_Z = "z_far"
+NEAR_Z = "z_near"
+SHARD = (X, FAR_Z, NEAR_Z)
+PLANE = (X, NEAR_Z)
 
 MOMENTUM = 0.9
 CLIP_RMS = 0.35
@@ -31,9 +33,18 @@
 
 def whole_rows(shard):
     slots, rows, rank = shard.shape
-    line = spread(shard, Z)
-    plane = spread(line, X)
-    return plane.reshape(-1, slots, rows, rank).transpose(1, 0, 2, 3).reshape(slots, -1, rank)
+    plane = spread(spread(shard, FAR_Z), PLANE)
+    plane = plane.reshape(lax.axis_size(X), lax.axis_size(NEAR_Z), -1, slots, rows, rank)
+    return plane.transpose(3, 0, 2, 1, 4, 5).reshape(slots, -1, rank)
+
+
+def summed_rows(partial):
+    slots, lines, rank = partial.shape
+    sizes = [lax.axis_size(a) for a in SHARD]
+    blocks = partial.reshape(slots, *sizes, -1, rank).transpose(1, 3, 2, 0, 4, 5)
+    blocks = blocks.reshape(sizes[0] * sizes[2], *blocks.shape[2:]).astype(BF16)
+    line = exchange(blocks, PLANE).astype(F32).sum(axis=0)
+    return exchange(line, FAR_Z).sum(axis=0)
 
 
 def inverse_factor_kernel(gram_ref, out_ref, work_ref):
@@ -98,9 +109,7 @@
     slots, rows_dev, cols = buffer.shape
     rank = right_basis.shape[-1]
     devices = lax.axis_size(SHARD)
-    near, far = lax.axis_size(Z), lax.axis_size(X)
     rows_all = rows_dev * devices
-    width = cols // devices
     count = layer_count[0]
     used = jnp.arange(slots, dtype=jnp.int32) < count
     keep = used[:, None, None]
@@ -129,10 +138,7 @@
     left = jnp.where(keep, clip * math.sqrt(rows_all) * ortho, 0.0).astype(BF16)
 
     partial = jnp.einsum("kij,kir->kjr", buffer, half_left, preferred_element_type=F32)
-    partial = partial.astype(BF16).reshape(slots, far, near * width, rank).transpose(1, 0, 2, 3)
-    line = exchange(partial, X).astype(F32).sum(axis=0)
-    line = line.reshape(slots, near, width, rank).transpose(1, 0, 2, 3)
-    right = exchange(line, Z).sum(axis=0)
+    right = summed_rows(partial)
     half_right = whole_rows(right.astype(BF16))
     colsq = jnp.sum(jnp.square(half_right.astype(F32)), axis=1, keepdims=True)
     right_step = jnp.where(keep, right * (math.sqrt(cols) * lax.rsqrt(colsq + 1.0)), 0.0)
@@ -143,7 +149,7 @@
 
 
 def solution(mesh):
-    split = Mesh(mesh.devices.reshape(4, 2, 4, 8), (*SEG, *SHARD))
+    split = Mesh(mesh.devices.reshape(4, 2, 4, 4, 2), (*SEG, *SHARD))
     specs = (P(SEG, SHARD, None), P(SEG, SHARD, None), P(SEG))
     outs = (P(SEG, SHARD, None),) * 3
     return jax.shard_map(body, mesh=split, in_specs=specs, out_specs=outs, check_vma=False)

time: 266 us -> 246 us (0.925)
  blocking collectives: 163 us -> 140 us
    all_to_all x6, blocking collectives: 163 us -> 140 us  [exchange(): return lax.all_to_all(blocks, axis, split_axis=0, concat_axis=0, tiled=True)]
where the time goes in v2:
time: 246 us; the launch traced here: 245 us
  blocking collectives  140 us (57%)
  waiting for transfers between devices  39.3 us (16%)
  matrix products  18.9 us (8%)
  starting transfers between devices  15.3 us (6%)
  Pallas kernels  12.5 us (5%)
  local copies, waits for them, and re-layouts  9.26 us (4%)
  other arithmetic  7.13 us (3%)
  between operations  2.83 us (1%)
    all_to_all x6, blocking collectives, exchange(): return lax.all_to_all(blocks, axis, split_axis=0, concat_axis=0, tiled=True)  140 us
    all_to_all x3, waiting for transfers between devices, exchange(): return lax.all_to_all(blocks, axis, split_axis=0, concat_axis=0, tiled=True)  39.3 us
    all_to_all x3, starting transfers between devices, exchange(): return lax.all_to_all(blocks, axis, split_axis=0, concat_axis=0, tiled=True)  15.3 us
    pallas_call x1, Pallas kernels, inverse_factor(): pl.pallas_call(inverse_factor_kernel, out_shape=jax.ShapeDtypeStruct(gram...  12.5 us
    dot_general x1, matrix products, body(): jnp.einsum('kij,kir->kjr', buffer, half_left, preferred_element_type=F32)  6.2 us
  transfers between devices with their start and end apart: 3, of which 2 were waited for; matrix products, arithmetic and copies ran while one was open for 2% of the time, Pallas kernels for 5%

profile of v2, /device:TPU:24, one launch (start us, length us, event | category | flops | bytes accessed | tf_op | source)
XLA Modules:
  0.0 245.2 jit_solution(2672844493689868130)
XLA Ops:
  0.6 0.9 broadcast_in_dim.85
  1.5 20.3 %all_to_all.45 = bf16[4,2,72,256]{3,2,1,0:T(8,128)(2,1)S(1)} all-to-all(bf16[4,2,72,256]{3,2,1,0:T(8,128)(2,1)S(1)} %broadcast_in_dim.85), channel_id=1, replica_groups=mesh['segment_0'=4,'segment_1'=2,'x'=4,'z_far'=4,'z_near'=2] {'z_far'}, dimensions={0} | all-to-all | bytes 589824 | tf_op jit(solution)/shard_map/all_to_all | solution.py:27
  21.8 1.6 broadcast_in_dim.86
  23.4 4.8 %all-to-all-start.1 = ((bf16[8,4,2,72,256]{4,3,2,1,0:T(8,128)(2,1)}), bf16[8,4,2,72,256]{4,3,2,1,0:T(8,128)(2,1)S(1)}, u32[]{:S(2)}, u32[]{:S(2)}) async-start(bf16[8,4,2,72,256]{4,3,2,1,0:T(8,128)(2,1)} %broadcast_in_dim.86), calls=%async_computation.1 | async-start | bytes 4718592 | tf_op jit(solution)/shard_map/all_to_all | solution.py:27
  28.2 4.0 %fusion = f32[2]{0:T(128)S(1)} fusion(bf16[2,576,2304]{2,1,0:T(8,128)(2,1)} %param.3), kind=kLoop, calls=%fused_computation.2 | loop fusion | flops 7962622 | bytes 5308424 | tf_op jit(solution)/shard_map/reduce_sum | solution.py:120
  32.2 23.5 %all-to-all-done.1 = bf16[8,4,2,72,256]{4,3,2,1,0:T(8,128)(2,1)S(1)} async-done(((bf16[8,4,2,72,256]{4,3,2,1,0:T(8,128)(2,1)}), bf16[8,4,2,72,256]{4,3,2,1,0:T(8,128)(2,1)S(1)}, u32[]{:S(2)}, u32[]{:S(2)}) %all-to-all-start.1) | async-done | bytes 2359328 | tf_op jit(solution)/shard_map/all_to_all | solution.py:27
  55.7 0.2 copy.14
  55.9 4.0 %fusion.7 = f32[2,576,256]{2,1,0:T(8,128)S(1)} fusion(bf16[2,576,2304]{2,1,0:T(8,128)(2,1)} %param.3, bf16[2,2304,256]{2,1,0:T(8,128)(2,1)S(1)} %bitcast.41), kind=kOutput, calls=%fused_computation.25 | convolution fusion | flops 1358954496 | bytes 8847360 | tf_op jit(solution)/shard_map/kij,kjr->kir/dot_general | solution.py:118
  59.9 2.3 convolution_select_fusion
  62.2 21.1 %all_to_all.46 = f32[32,16,256]{2,1,0:T(8,128)S(1)} all-to-all(f32[32,16,256]{2,1,0:T(8,128)S(1)} %bitcast.44), channel_id=1, replica_groups=mesh['segment_0'=4,'segment_1'=2,'x'=4,'z_far'=4,'z_near'=2] {'x','z_far..., dimensions={0} | all-to-all | bytes 1048576 | tf_op jit(solution)/shard_map/all_to_all | solution.py:27
  83.4 0.9 broadcast_in_dim.88
  84.2 5.8 %all-to-all-start.3 = ((f32[32,16,256]{2,1,0:T(8,128)}), f32[32,16,256]{2,1,0:T(8,128)S(1)}, u32[]{:S(2)}, u32[]{:S(2)}) async-start(f32[32,16,256]{2,1,0:T(8,128)} %broadcast_in_dim.88), calls=%async_computation.3 | async-start | bytes 1048576 | tf_op jit(solution)/shard_map/all_to_all | solution.py:27
  90.7 15.8 %all-to-all-done.3 = f32[32,16,256]{2,1,0:T(8,128)S(1)} async-done(((f32[32,16,256]{2,1,0:T(8,128)}), f32[32,16,256]{2,1,0:T(8,128)S(1)}, u32[]{:S(2)}, u32[]{:S(2)}) %all-to-all-start.3) | async-done | bytes 524320 | tf_op jit(solution)/shard_map/all_to_all | solution.py:27
  106.5 0.2 slice_reduce_fusion.1
  106.7 0.6 select_reduce_fusion
  107.3 0.6 compare_select_fusion
  107.9 0.6 broadcast_in_dim.98
  108.6 4.7 %all-to-all-start.8 = ((f32[8,8,128]{2,1,0:T(8,128)}), f32[8,8,128]{2,1,0:T(8,128)S(1)}, u32[]{:S(2)}, u32[]{:S(2)}) async-start(f32[8,8,128]{2,1,0:T(8,128)} %broadcast_in_dim.98), calls=%async_computation.8 | async-start | bytes 65536 | tf_op jit(solution)/shard_map/all_to_all | solution.py:27
  113.2 0.2 and_select_fusion.gram_ref
  113.4 12.5 %inverse_factor.1 = f32[2,256,256]{2,1,0:T(8,128)S(1)} custom-call(f32[2,256,256]{2,1,0:T(8,128)S(1)} %and_select_fusion.gram_ref), custom_call_target="tpu_custom_call" | custom-call | tf_op jit(solution)/shard_map/inverse_factor/pallas_call | solution.py:97
  125.9 0.0 all-to-all-done.8
  125.9 0.6 fusion.6
  127.9 2.0 select_convert_fusion
  129.9 0.0 copy-start
  129.9 0.8 copy-done
  130.7 6.2 %fusion.3 = bf16[2,2304,256]{1,2,0:T(8,128)(2,1)} fusion(bf16[2,576,2304]{2,1,0:T(8,128)(2,1)} %param.3, bf16[2,576,256]{2,1,0:T(8,128)(2,1)S(1)} %get-tuple-element.8), kind=kOutput, calls=%fused_computation.8 | convolution fusion | flops 1360134144 | bytes 8257536 | tf_op jit(solution)/shard_map/kij,kir->kjr/dot_general | solution.py:140
  136.9 2.8 %copy.15 = bf16[2,2304,256]{2,1,0:T(8,128)(2,1)S(1)} copy(bf16[2,2304,256]{1,2,0:T(8,128)(2,1)} %fusion.3) | data formatting | bytes 4718592 | tf_op jit(solution)/shard_map/convert_element_type | solution.py:45
  139.8 0.2 copy.16
  140.0 34.1 %all_to_all.47 = bf16[8,4,2,72,256]{4,3,2,1,0:T(8,128)(2,1)S(1)} all-to-all(bf16[8,4,2,72,256]{4,3,2,1,0:T(8,128)(2,1)S(1)} %bitcast.37), channel_id=1, replica_groups=mesh['segment_0'=4,'segment_1'=2,'x'=4,'z_far'=4,'z_near'=2] {'x','z_near'}, dimensions={0} | all-to-all | bytes 4718592 | tf_op jit(solution)/shard_map/all_to_all | solution.py:27
  174.1 0.3 convert_reduce_fusion
  174.4 19.9 %all_to_all.48 = f32[4,2,72,256]{3,2,1,0:T(8,128)S(1)} all-to-all(f32[4,2,72,256]{3,2,1,0:T(8,128)S(1)} %convert_reduce_fusion), channel_id=1, replica_groups=mesh['segment_0'=4,'segment_1'=2,'x'=4,'z_far'=4,'z_near'=2] {'z_far'}, dimensions={0} | all-to-all | bytes 1179648 | tf_op jit(solution)/shard_map/all_to_all | solution.py:27
  194.3 0.0 slice-start
  194.4 12.9 %all_to_all.49 = bf16[4,2,72,256]{3,2,1,0:T(8,128)(2,1)S(1)} all-to-all(bf16[4,2,72,256]{3,2,1,0:T(8,128)(2,1)S(1)} %broadcast_in_dim.91), channel_id=1, replica_groups=mesh['segment_0'=4,'segment_1'=2,'x'=4,'z_far'=4,'z_near'=2] {'z_far'}, dimensions={0} | all-to-all | bytes 589824 | tf_op jit(solution)/shard_map/all_to_all | solution.py:27
  207.3 0.2 broadcast_in_dim.92
  207.5 0.0 slice-start.1
  207.5 31.8 %all_to_all.50 = bf16[8,4,2,72,256]{4,3,2,1,0:T(8,128)(2,1)S(1)} all-to-all(bf16[8,4,2,72,256]{4,3,2,1,0:T(8,128)(2,1)S(1)} %broadcast_in_dim.92), channel_id=1, replica_groups=mesh['segment_0'=4,'segment_1'=2,'x'=4,'z_far'=4,'z_near'=2] {'x','z_near'}, dimensions={0} | all-to-all | bytes 4718592 | tf_op jit(solution)/shard_map/all_to_all | solution.py:27
  239.3 0.5 multiply_reduce_fusion
  239.8 0.0 copy-start.1
  239.8 0.2 copy.17
  240.1 0.7 multiply_select_fusion
  240.8 0.0 slice-done
  240.8 0.0 slice-done.1
  240.8 0.1 copy-done.1
  240.9 4.3 %fusion.2 = bf16[2,576,2304]{2,1,0:T(8,128)(2,1)} fusion(bf16[2,576,2304]{2,1,0:T(8,128)(2,1)S(1)} %bitcast.39, bf16[2,2304,256]{2,1,0:T(8,128)(2,1)S(1)} %bitcast.40, pred[2]{0:T(512)(128)(4,1)S(1)} %iota_compare_fusion.2, bf16[2,576,256]{2,1,0:T(8,128)(2,1)S(1)} %copy-done.1), kind=kOutput, calls=%fused_computation.4 | convolution fusion | flops 1372225536 | bytes 13565954 | tf_op jit(solution)/shard_map/kir,kjr->kij/dot_general | solution.py:146
  (9 shorter events, 0.2 us)
Async XLA Ops:
  23.4 32.3 %all-to-all-start.1 = ((bf16[8,4,2,72,256]{4,3,2,1,0:T(8,128)(2,1)}), bf16[8,4,2,72,256]{4,3,2,1,0:T(8,128)(2,1)S(1)}, u32[]{:S(2)}, u32[]{:S(2)}) async-start(bf16[8,4,2,72,256]{4,3,2,1,0:T(8,128)(2,1)} %broadcast_in_dim.86), calls=%async_computation.1 | async-start | bytes 4718592 | tf_op jit(solution)/shard_map/all_to_all | solution.py:27
  84.2 22.3 %all-to-all-start.3 = ((f32[32,16,256]{2,1,0:T(8,128)}), f32[32,16,256]{2,1,0:T(8,128)S(1)}, u32[]{:S(2)}, u32[]{:S(2)}) async-start(f32[32,16,256]{2,1,0:T(8,128)} %broadcast_in_dim.88), calls=%async_computation.3 | async-start | bytes 1048576 | tf_op jit(solution)/shard_map/all_to_all | solution.py:27
  108.6 17.3 %all-to-all-start.8 = ((f32[8,8,128]{2,1,0:T(8,128)}), f32[8,8,128]{2,1,0:T(8,128)S(1)}, u32[]{:S(2)}, u32[]{:S(2)}) async-start(f32[8,8,128]{2,1,0:T(8,128)} %broadcast_in_dim.98), calls=%async_computation.8 | async-start | bytes 65536 | tf_op jit(solution)/shard_map/all_to_all | solution.py:27
  129.9 0.8 copy-start
  194.3 46.5 %slice-start = ((s8[5308416]{0:T(1024)(128)(4,1)}), s8[4194304]{0:T(1024)(128)(4,1)S(1)}, s32[]{:S(2)}) async-start(s8[5308416]{0:T(1024)(128)(4,1)} %bitcast.38), calls=%async_computation.9 | async-start | bytes 8388608
  207.5 33.3 %slice-start.1 = ((s8[5308416]{0:T(1024)(128)(4,1)}), s8[1114112]{0:T(1024)(128)(4,1)S(1)}, s32[]{:S(2)}) async-start(s8[5308416]{0:T(1024)(128)(4,1)} %bitcast.38), calls=%async_computation.10 | async-start | bytes 2228224
  239.8 1.1 copy-start.1

commit v3 on v2

v3 whole, which is shorter than its diff:
```python
import math

import jax
import jax.numpy as jnp
from jax import lax
from jax.experimental import pallas as pl
from jax.experimental.pallas import tpu as pltpu
from jax.sharding import Mesh
from jax.sharding import PartitionSpec as P

SEG = ("segment_0", "segment_1")
X = "x"
FAR_Z = "z_far"
NEAR_Z = "z_near"
SHARD = (X, FAR_Z, NEAR_Z)
PLANE = (X, NEAR_Z)

MOMENTUM = 0.9
CLIP_RMS = 0.35
SQUARE_FLOOR = 0.0625
BLOCK = 16
F32 = jnp.float32
BF16 = jnp.bfloat16


def exchange(blocks, axis):
    return lax.all_to_all(blocks, axis, split_axis=0, concat_axis=0, tiled=True)


def spread(value, axis):
    return exchange(jnp.broadcast_to(value, (lax.axis_size(axis), *value.shape)), axis)


def whole_rows(shard):
    slots, rows, rank = shard.shape
    plane = spread(spread(shard, FAR_Z), PLANE)
    plane = plane.reshape(lax.axis_size(X), lax.axis_size(NEAR_Z), -1, slots, rows, rank)
    return plane.transpose(3, 0, 2, 1, 4, 5).reshape(slots, -1, rank)


def summed_rows(blocks):
    line = exchange(blocks, PLANE).astype(F32).sum(axis=0)
    return exchange(line, FAR_Z).sum(axis=0)


def project_kernel(square_ref, block_ref, basis_ref, proj_ref, gram_ref):
    slot, step = pl.program_id(0), pl.program_id(1)
    proj = jnp.dot(block_ref[0], basis_ref[0], preferred_element_type=F32)
    proj_ref[0] = proj
    gram = lax.dot_general(
        proj, proj, (((0,), (0,)), ((), ())), precision=lax.Precision.HIGHEST, preferred_element_type=F32
    )
    total = jnp.where(step == 0, gram, gram_ref[0] + gram)
    row = lax.broadcasted_iota(jnp.int32, total.shape, 0)
    col = lax.broadcasted_iota(jnp.int32, total.shape, 1)
    corner = (row == 0) & (col == total.shape[1] - 1)
    gram_ref[0] = jnp.where(corner, square_ref[slot], total)


def project(buffer, basis, squares, steps=2):
    slots, rows, cols = buffer.shape
    rank = basis.shape[-1]
    part = rows // steps
    return pl.pallas_call(
        project_kernel,
        grid=(slots, steps),
        in_specs=[
            pl.BlockSpec(memory_space=pltpu.SMEM),
            pl.BlockSpec((1, part, cols), lambda s, i: (s, i, 0)),
            pl.BlockSpec((1, cols, rank), lambda s, i: (s, 0, 0)),
        ],
        out_specs=[
            pl.BlockSpec((1, part, rank), lambda s, i: (s, i, 0)),
            pl.BlockSpec((1, rank, rank), lambda s, i: (s, 0, 0)),
        ],
        out_shape=[
            jax.ShapeDtypeStruct((slots, rows, rank), F32),
            jax.ShapeDtypeStruct((slots, rank, rank), F32),
        ],
        compiler_params=pltpu.CompilerParams(vmem_limit_bytes=24 << 20),
        name="project",
    )(squares, buffer, basis)


def eliminate(work_ref, slots, n):
    b = BLOCK
    tiles = 2 * n // 128
    sub = lax.broadcasted_iota(jnp.int32, (b, 128), 0)
    for j in range(n // b):
        lo, hi = j * b, (j + 1) * b
        panels = []
        cols = []
        for s in range(slots):
            panel = work_ref[s, lo:hi, :]
            panels.append(panel)
            cols.append([jnp.broadcast_to(panel[:, lo + k : lo + k + 1], (b, 128)) for k in range(b)])
        for k in range(b):
            for s in range(slots):
                c = cols[s]
                inv = lax.rsqrt(jnp.broadcast_to(c[k][k : k + 1], (b, 128)))
                scaled = c[k] * inv
                below = jnp.where(sub > k, scaled, 0.0)
                for i in range(k + 1, b):
                    c[i] = c[i] - below * jnp.broadcast_to(scaled[i : i + 1], (b, 128))
                p = panels[s]
                pivot = p[k : k + 1] * jnp.concatenate([inv[:1]] * tiles, axis=1)
                below_all = jnp.concatenate([below] * tiles, axis=1)
                at_k = jnp.concatenate([sub == k] * tiles, axis=1)
                pivot_all = jnp.broadcast_to(pivot, (b, 2 * n))
                panels[s] = jnp.where(at_k, pivot_all, p - below_all * pivot_all)
        for s in range(slots):
            work_ref[s, lo:hi, :] = panels[s]
            if hi < n:
                update = lax.dot_general(
                    panels[s][:, hi:n], panels[s], (((0,), (0,)), ((), ())),
                    precision=lax.Precision.HIGHEST, preferred_element_type=F32,
                )
                work_ref[s, hi:, :] = work_ref[s, hi:, :] - update


def factor_kernel(gram_ref, proj_ref, buffer_ref, ortho_ref, half_ref, blocks_ref, work_ref, block_ref, sum_ref, sems):
    slots, rows, n = proj_ref.shape
    cols = block_ref.shape[-1]
    near_blocks, far, _, width, _ = blocks_ref.shape
    loads = [pltpu.make_async_copy(buffer_ref.at[s], block_ref.at[s], sems.at[s]) for s in range(slots)]
    for load in loads:
        load.start()
    row = lax.broadcasted_iota(jnp.int32, (n, n), 0)
    col = lax.broadcasted_iota(jnp.int32, (n, n), 1)
    for s in range(slots):
        gram = gram_ref[s * n : (s + 1) * n, :]
        mirror = jnp.broadcast_to(gram[n - 1 :, :1], (n, n))
        work_ref[s, :, :n] = jnp.where((row == 0) & (col == n - 1), mirror, gram)
        work_ref[s, :, n:] = (row == col).astype(F32)
    eliminate(work_ref, slots, n)
    for s in range(slots):
        ortho = lax.dot_general(
            proj_ref[s], work_ref[s, :, n:], (((1,), (1,)), ((), ())),
            precision=lax.Precision.HIGHEST, preferred_element_type=F32,
        )
        ortho_ref[s] = ortho
        half_ref[s] = ortho.astype(BF16)
        loads[s].wait()
        half = half_ref[s]
        for c in range(0, cols, n):
            sum_ref[c : c + n, :] = lax.dot_general(
                block_ref[s, :, c : c + n], half, (((0,), (0,)), ((), ())), preferred_element_type=F32
            )
        near = lax.axis_size(NEAR_Z)
        for c in range(cols // width):
            x, z = divmod(c, far * near)
            f, m = divmod(z, near)
            blocks_ref[x * near + m, f, s] = sum_ref[c * width : (c + 1) * width, :].astype(BF16)


def factor(gram, proj, buffer):
    slots, rows, rank = proj.shape
    cols = buffer.shape[-1]
    devices = lax.axis_size(SHARD)
    far = lax.axis_size(FAR_Z)
    vmem = pl.BlockSpec(memory_space=pltpu.VMEM)
    return pl.pallas_call(
        factor_kernel,
        in_specs=[vmem, vmem, pl.BlockSpec(memory_space=pl.ANY)],
        out_specs=[vmem, vmem, vmem],
        out_shape=[
            jax.ShapeDtypeStruct((slots, rows, rank), F32),
            jax.ShapeDtypeStruct((slots, rows, rank), BF16),
            jax.ShapeDtypeStruct((devices // far, far, slots, cols // devices, rank), BF16),
        ],
        scratch_shapes=[
            pltpu.VMEM((slots, rank, 2 * rank), F32),
            pltpu.VMEM((slots, rows, cols), BF16),
            pltpu.VMEM((cols, rank), F32),
            pltpu.SemaphoreType.DMA((slots,)),
        ],
        compiler_params=pltpu.CompilerParams(vmem_limit_bytes=32 << 20),
        name="factor",
    )(gram, proj, buffer)


def body(buffer, right_basis, layer_count):
    slots, rows_dev, cols = buffer.shape
    rank = right_basis.shape[-1]
    devices = lax.axis_size(SHARD)
    rows_all = rows_dev * devices
    count = layer_count[0]
    used = jnp.arange(slots, dtype=jnp.int32) < count
    keep = used[:, None, None]

    basis = whole_rows(right_basis)
    per_slot = jnp.sum(jnp.square(buffer.astype(F32)), axis=(1, 2))
    proj, gram = project(buffer, basis, per_slot)
    part = exchange(gram.reshape(devices, -1, rank), SHARD).sum(axis=0)
    gram = spread(part, SHARD).reshape(slots * rank, rank)
    ortho, half_left, blocks = factor(gram, proj, buffer)
    right = summed_rows(blocks)

    squares = jnp.sum(jnp.where(used, gram[::rank, rank - 1], 0.0))
    elements = count.astype(F32) * float(rows_all * cols)
    totals = lax.psum(jnp.stack([squares, elements]), SEG)
    clip = jnp.minimum(1.0, CLIP_RMS * lax.rsqrt(jnp.maximum(totals[0] / totals[1], SQUARE_FLOOR)))
    left = jnp.where(keep, clip * math.sqrt(rows_all) * ortho, 0.0).astype(BF16)

    half_right = whole_rows(right.astype(BF16))
    colsq = jnp.sum(jnp.square(half_right.astype(F32)), axis=1, keepdims=True)
    right_step = jnp.where(keep, right * (math.sqrt(cols) * lax.rsqrt(colsq + 1.0)), 0.0)

    correction = jnp.einsum("kir,kjr->kij", half_left, half_right, preferred_element_type=F32)
    moment = jnp.where(keep, buffer - (1.0 - MOMENTUM) * correction, 0.0).astype(BF16)
    return moment, left, right_step


def solution(mesh):
    split = Mesh(mesh.devices.reshape(4, 2, 4, 4, 2), (*SEG, *SHARD))
    specs = (P(SEG, SHARD, None), P(SEG, SHARD, None), P(SEG))
    outs = (P(SEG, SHARD, None),) * 3
    return jax.shard_map(body, mesh=split, in_specs=specs, out_specs=outs, check_vma=False)
```

time: 246 us -> 243 us (0.988)
  Pallas kernels: 12.5 us -> 24.9 us
  matrix products: 18.9 us -> 6.79 us
  starting transfers between devices: 15.3 us -> 9.17 us
  waiting for transfers between devices: 39.3 us -> 35.2 us
  local copies, waits for them, and re-layouts: 9.26 us -> 11.9 us
  other arithmetic: 7.13 us -> 9.73 us
    dot_general x4 -> x0, matrix products: 14.6 us -> none  [the longest x1 6.2 us: body(): jnp.einsum('kij,kir->kjr', buffer, half_left, preferred_element_type=F32)]
    pallas_call x1 -> x2, Pallas kernels: 12.5 us -> 24.9 us  [the longest x1 17.2 us: factor(): pl.pallas_call(factor_kernel, in_specs=[vmem, vmem, pl.BlockSpec(memory_s...]
    psum x0 -> x1, blocking collectives: none -> 10.8 us  [body(): totals = lax.psum(jnp.stack([squares, elements]), SEG)]
    all_to_all x6, blocking collectives: 140 us -> 131 us  [exchange(): return lax.all_to_all(blocks, axis, split_axis=0, concat_axis=0, tiled=True)]
    all_to_all x3 -> x2, starting transfers between devices: 15.3 us -> 9.17 us  [exchange(): return lax.all_to_all(blocks, axis, split_axis=0, concat_axis=0, tiled=True)]
    unnamed x8 -> x4, local copies, waits for them, and re-layouts: 0.91 us -> 5 us
    all_to_all x3 -> x2, waiting for transfers between devices: 39.3 us -> 35.2 us  [exchange(): return lax.all_to_all(blocks, axis, split_axis=0, concat_axis=0, tiled=True)]
    convert_element_type x2 -> x0, local copies, waits for them, and re-layouts: 3.02 us -> none  [summed_rows(): blocks = blocks.reshape(sizes[0] * sizes[2], *blocks.shape[2:]).astype(BF16)]
  transfers between devices with their start and end apart: 3 -> 2, of which waited for: 2 -> 2; matrix products, arithmetic and copies ran while one was open for 2% -> 3% of each run, Pallas kernels for 5% -> 0%
where the time goes in v3:
time: 243 us; the launch traced here: 242 us
  blocking collectives  141 us (58%)
  waiting for transfers between devices  35.2 us (14%)
  Pallas kernels  24.9 us (10%)
  local copies, waits for them, and re-layouts  11.9 us (5%)
  other arithmetic  9.73 us (4%)
  starting transfers between devices  9.17 us (4%)
  matrix products  6.79 us (3%)
  between operations  2.77 us (1%)
    all_to_all x6, blocking collectives, exchange(): return lax.all_to_all(blocks, axis, split_axis=0, concat_axis=0, tiled=True)  131 us
    all_to_all x2, waiting for transfers between devices, exchange(): return lax.all_to_all(blocks, axis, split_axis=0, concat_axis=0, tiled=True)  35.2 us
    pallas_call x1, Pallas kernels, factor(): pl.pallas_call(factor_kernel, in_specs=[vmem, vmem, pl.BlockSpec(memory_s...  17.2 us
    psum x1, blocking collectives, body(): totals = lax.psum(jnp.stack([squares, elements]), SEG)  10.8 us
    all_to_all x2, starting transfers between devices, exchange(): return lax.all_to_all(blocks, axis, split_axis=0, concat_axis=0, tiled=True)  9.17 us
    pallas_call x1, Pallas kernels, project(): pl.pallas_call(project_kernel, grid=(slots, steps), in_specs=[pl.BlockSpe...  7.67 us
    dot_general x1, matrix products, body(): jnp.einsum('kir,kjr->kij', half_left, half_right, preferred_element_type=...  6.79 us
    unnamed x4, local copies, waits for them, and re-layouts  5 us
  transfers between devices with their start and end apart: 2, of which 2 were waited for; matrix products, arithmetic and copies ran while one was open for 3% of the time, Pallas kernels for 0%

profile of v3, /device:TPU:24, one launch (start us, length us, event | category | flops | bytes accessed | tf_op | source)
XLA Modules:
  0.0 242.0 jit_solution(6180789936213746980)
XLA Ops:
  0.6 0.9 broadcast_in_dim.58
  1.5 20.3 %all_to_all.40 = bf16[4,2,72,256]{3,2,1,0:T(8,128)(2,1)S(1)} all-to-all(bf16[4,2,72,256]{3,2,1,0:T(8,128)(2,1)S(1)} %broadcast_in_dim.58), channel_id=1, replica_groups=mesh['segment_0'=4,'segment_1'=2,'x'=4,'z_far'=4,'z_near'=2] {'z_far'}, dimensions={0} | all-to-all | bytes 589824 | tf_op jit(solution)/shard_map/all_to_all | solution.py:27
  21.8 1.6 broadcast_in_dim.59
  23.4 4.8 %all-to-all-start.1 = ((bf16[8,4,2,72,256]{4,3,2,1,0:T(8,128)(2,1)}), bf16[8,4,2,72,256]{4,3,2,1,0:T(8,128)(2,1)S(1)}, u32[]{:S(2)}, u32[]{:S(2)}) async-start(bf16[8,4,2,72,256]{4,3,2,1,0:T(8,128)(2,1)} %broadcast_in_dim.59), calls=%async_computation.1 | async-start | bytes 4718592 | tf_op jit(solution)/shard_map/all_to_all | solution.py:27
  28.2 4.0 %fusion.square_ref = f32[2]{0:T(128)S(1)} fusion(bf16[2,576,2304]{2,1,0:T(8,128)(2,1)} %buffer_ref.1), kind=kLoop, calls=%fused_computation.2 | loop fusion | flops 7962622 | bytes 5308424 | tf_op jit(solution)/shard_map/reduce_sum | solution.py:192
  32.2 23.5 %all-to-all-done.1 = bf16[8,4,2,72,256]{4,3,2,1,0:T(8,128)(2,1)S(1)} async-done(((bf16[8,4,2,72,256]{4,3,2,1,0:T(8,128)(2,1)}), bf16[8,4,2,72,256]{4,3,2,1,0:T(8,128)(2,1)S(1)}, u32[]{:S(2)}, u32[]{:S(2)}) %all-to-all-start.1) | async-done | bytes 2359328 | tf_op jit(solution)/shard_map/all_to_all | solution.py:27
  55.7 0.2 copy.8
  55.9 0.0 copy-start
  55.9 2.5 %copy-done = bf16[2,576,2304]{2,1,0:T(8,128)(2,1)S(1)} copy-done((bf16[2,576,2304]{2,1,0:T(8,128)(2,1)S(1)}, bf16[2,576,2304]{2,1,0:T(8,128)(2,1)}, u32[]{:S(2)}) %copy-start) | copy-done | bytes 5308440
  58.4 7.7 %project.1 = (f32[2,576,256]{2,1,0:T(8,128)S(1)}, f32[2,256,256]{2,1,0:T(8,128)S(1)}) custom-call(f32[2]{0:T(128)S(1)} %fusion.square_ref, bf16[2,576,2304]{2,1,0:T(8,128)(2,1)S(1)} %copy-done, bf16[2,2304,256]{2,1,0:T(8,128)(2,1)S(1)} %bitcast.19), custom_call_target="tpu_custom_call" | custom-call | tf_op jit(solution)/shard_map/project/pallas_call | solution.py:64
  66.1 21.1 %all_to_all.41 = f32[32,16,256]{2,1,0:T(8,128)S(1)} all-to-all(f32[32,16,256]{2,1,0:T(8,128)S(1)} %bitcast.22), channel_id=1, replica_groups=mesh['segment_0'=4,'segment_1'=2,'x'=4,'z_far'=4,'z_near'=2] {'x','z_far..., dimensions={0} | all-to-all | bytes 1048576 | tf_op jit(solution)/shard_map/all_to_all | solution.py:27
  87.2 0.1 broadcast_in_dim.60
  87.3 22.1 %all_to_all.42 = f32[32,16,256]{2,1,0:T(8,128)S(1)} all-to-all(f32[32,16,256]{2,1,0:T(8,128)S(1)} %broadcast_in_dim.60), channel_id=1, replica_groups=mesh['segment_0'=4,'segment_1'=2,'x'=4,'z_far'=4,'z_near'=2] {'x','z_far..., dimensions={0} | all-to-all | bytes 1048576 | tf_op jit(solution)/shard_map/all_to_all | solution.py:27
  109.4 0.0 copy-start.1
  109.4 2.5 %copy-done.1 = bf16[2,576,2304]{2,1,0:T(8,128)(2,1)S(1)} copy-done((bf16[2,576,2304]{2,1,0:T(8,128)(2,1)S(1)}, bf16[2,576,2304]{2,1,0:T(8,128)(2,1)}, u32[]{:S(2)}) %copy-start.1) | copy-done | bytes 5308440
  111.9 17.2 %factor.1 = (f32[2,576,256]{2,1,0:T(8,128)S(1)}, bf16[2,576,256]{2,1,0:T(8,128)(2,1)S(1)}, bf16[8,4,2,72,256]{4,3,2,1,0:T(8,128)(2,1)S(1)}) custom-call(f32[512,256]{1,0:T(8,128)S(1)} %bitcast.20, f32[2,576,256]{2,1,0:T(8,128)S(1)} %get-tuple-element.9.proj_ref, bf16[2,576,2304]{2,1,0:T(8,128)(2,1)S(1)} %copy-done.1), custom_call_target="tpu_custom_call" | custom-call | tf_op jit(solution)/shard_map/factor/pallas_call | solution.py:162
  129.1 32.8 %all_to_all.43 = bf16[8,4,2,72,256]{4,3,2,1,0:T(8,128)(2,1)S(1)} all-to-all(bf16[8,4,2,72,256]{4,3,2,1,0:T(8,128)(2,1)S(1)} %get-tuple-element.11), channel_id=1, replica_groups=mesh['segment_0'=4,'segment_1'=2,'x'=4,'z_far'=4,'z_near'=2] {'x','z_near'}, dimensions={0} | all-to-all | bytes 4718592 | tf_op jit(solution)/shard_map/all_to_all | solution.py:27
  161.9 0.3 convert_reduce_fusion
  162.2 20.2 %all_to_all.44 = f32[4,2,72,256]{3,2,1,0:T(8,128)S(1)} all-to-all(f32[4,2,72,256]{3,2,1,0:T(8,128)S(1)} %convert_reduce_fusion), channel_id=1, replica_groups=mesh['segment_0'=4,'segment_1'=2,'x'=4,'z_far'=4,'z_near'=2] {'z_far'}, dimensions={0} | all-to-all | bytes 1179648 | tf_op jit(solution)/shard_map/all_to_all | solution.py:27
  182.4 14.3 %all_to_all.45 = bf16[4,2,72,256]{3,2,1,0:T(8,128)(2,1)S(1)} all-to-all(bf16[4,2,72,256]{3,2,1,0:T(8,128)(2,1)S(1)} %broadcast_in_dim.61), channel_id=1, replica_groups=mesh['segment_0'=4,'segment_1'=2,'x'=4,'z_far'=4,'z_near'=2] {'z_far'}, dimensions={0} | all-to-all | bytes 589824 | tf_op jit(solution)/shard_map/all_to_all | solution.py:27
  196.8 1.6 broadcast_in_dim.62
  198.4 4.4 %all-to-all-start.7 = ((bf16[8,4,2,72,256]{4,3,2,1,0:T(8,128)(2,1)}), bf16[8,4,2,72,256]{4,3,2,1,0:T(8,128)(2,1)}, u32[]{:S(2)}, u32[]{:S(2)}) async-start(bf16[8,4,2,72,256]{4,3,2,1,0:T(8,128)(2,1)} %broadcast_in_dim.62), calls=%async_computation.7 | async-start | bytes 4718592 | tf_op jit(solution)/shard_map/all_to_all | solution.py:27
  203.4 0.1 slice.9
  203.5 0.1 reduce.1
  203.6 0.6 select_reduce_fusion
  204.2 0.6 pad_maximum_fusion
  204.9 10.8 %psum.7 = f32[2]{0:T(128)S(1)} all-reduce(f32[2]{0:T(128)S(1)} %pad_maximum_fusion), channel_id=1, replica_groups=mesh['segment_0'=4,'segment_1'=2,'x'=4,'z_far'=4,'z_near'=2] {'segment_0..., use_global_device_ids=true, to_apply=%region_5.6 | all-reduce | flops 2 | bytes 16 | tf_op jit(solution)/shard_map/psum | solution.py:201
  215.6 0.6 fusion.3
  217.6 1.0 select_convert_fusion
  218.7 11.7 %all-to-all-done.7 = bf16[8,4,2,72,256]{4,3,2,1,0:T(8,128)(2,1)} async-done(((bf16[8,4,2,72,256]{4,3,2,1,0:T(8,128)(2,1)}), bf16[8,4,2,72,256]{4,3,2,1,0:T(8,128)(2,1)}, u32[]{:S(2)}, u32[]{:S(2)}) %all-to-all-start.7) | async-done | bytes 2359328 | tf_op jit(solution)/shard_map/all_to_all | solution.py:27
  230.4 2.2 multiply_reduce_fusion
  232.6 1.8 copy.9
  234.5 0.7 multiply_select_fusion
  235.2 6.8 %fusion.2 = bf16[2,576,2304]{2,1,0:T(8,128)(2,1)} fusion(bf16[2,576,2304]{2,1,0:T(8,128)(2,1)} %buffer_ref.1, bf16[2,576,256]{2,1,0:T(8,128)(2,1)S(1)} %get-tuple-element.10, bf16[2,2304,256]{2,1,0:T(8,128)(2,1)S(1)} %bitcast.24, pred[2]{0:T(512)(128)(4,1)S(1)} %iota_compare_fusion), kind=kOutput, calls=%fused_computation.4 | convolution fusion | flops 1372225536 | bytes 13565954 | tf_op jit(solution)/shard_map/kir,kjr->kij/dot_general | solution.py:209
  (6 shorter events, 0.1 us)
Async XLA Ops:
  23.4 32.3 %all-to-all-start.1 = ((bf16[8,4,2,72,256]{4,3,2,1,0:T(8,128)(2,1)}), bf16[8,4,2,72,256]{4,3,2,1,0:T(8,128)(2,1)S(1)}, u32[]{:S(2)}, u32[]{:S(2)}) async-start(bf16[8,4,2,72,256]{4,3,2,1,0:T(8,128)(2,1)} %broadcast_in_dim.59), calls=%async_computation.1 | async-start | bytes 4718592 | tf_op jit(solution)/shard_map/all_to_all | solution.py:27
  55.9 2.5 %copy-start = (bf16[2,576,2304]{2,1,0:T(8,128)(2,1)S(1)}, bf16[2,576,2304]{2,1,0:T(8,128)(2,1)}, u32[]{:S(2)}) copy-start(bf16[2,576,2304]{2,1,0:T(8,128)(2,1)} %buffer_ref.1) | copy-start | bytes 15925252
  109.4 2.5 %copy-start.1 = (bf16[2,576,2304]{2,1,0:T(8,128)(2,1)S(1)}, bf16[2,576,2304]{2,1,0:T(8,128)(2,1)}, u32[]{:S(2)}) copy-start(bf16[2,576,2304]{2,1,0:T(8,128)(2,1)} %buffer_ref.1) | copy-start | bytes 15925252
  198.4 32.0 %all-to-all-start.7 = ((bf16[8,4,2,72,256]{4,3,2,1,0:T(8,128)(2,1)}), bf16[8,4,2,72,256]{4,3,2,1,0:T(8,128)(2,1)}, u32[]{:S(2)}, u32[]{:S(2)}) async-start(bf16[8,4,2,72,256]{4,3,2,1,0:T(8,128)(2,1)} %broadcast_in_dim.62), calls=%async_computation.7 | async-start | bytes 4718592 | tf_op jit(solution)/shard_map/all_to_all | solution.py:27

commit v4 on v3

--- a/solution.py
+++ b/solution.py
@@ -43,57 +43,78 @@
     return exchange(line, FAR_Z).sum(axis=0)
 
 
-def project_kernel(square_ref, block_ref, basis_ref, proj_ref, gram_ref):
-    slot, step = pl.program_id(0), pl.program_id(1)
-    proj = jnp.dot(block_ref[0], basis_ref[0], preferred_element_type=F32)
-    proj_ref[0] = proj
-    gram = lax.dot_general(
-        proj, proj, (((0,), (0,)), ((), ())), precision=lax.Precision.HIGHEST, preferred_element_type=F32
-    )
-    total = jnp.where(step == 0, gram, gram_ref[0] + gram)
-    row = lax.broadcasted_iota(jnp.int32, total.shape, 0)
-    col = lax.broadcasted_iota(jnp.int32, total.shape, 1)
-    corner = (row == 0) & (col == total.shape[1] - 1)
-    gram_ref[0] = jnp.where(corner, square_ref[slot], total)
-
-
-def project(buffer, basis, squares, steps=2):
+def halves(value):
+    high = value.astype(BF16)
+    return high, (value - high.astype(F32)).astype(BF16)
+
+
+def dot(a, b, dims):
+    return lax.dot_general(a, b, (dims, ((), ())), preferred_element_type=F32)
+
+
+VMEM = pl.BlockSpec(memory_space=pltpu.VMEM)
+
+
+HBM = pl.BlockSpec(memory_space=pltpu.HBM)
+
+
+def project_kernel(square_ref, buffer_ref, basis_ref, proj_ref, gram_ref, block_ref, sems):
+    slots, rows, n = proj_ref.shape
+    parts = sems.shape[1]
+    part = rows // parts
+
+    def load(s, i):
+        at = pl.ds(i * part, part)
+        return pltpu.make_async_copy(buffer_ref.at[s, at], block_ref.at[s, at], sems.at[s, i])
+
+    for s in range(slots):
+        for i in range(parts):
+            load(s, i).start()
+    row = lax.broadcasted_iota(jnp.int32, (n, n), 0)
+    col = lax.broadcasted_iota(jnp.int32, (n, n), 1)
+    for s in range(slots):
+        for i in range(parts):
+            load(s, i).wait()
+            lines = slice(i * part, (i + 1) * part)
+            proj_ref[s, lines, :] = jnp.dot(block_ref[s, lines, :], basis_ref[s], preferred_element_type=F32)
+        high, low = halves(proj_ref[s])
+        cross = dot(high, low, ((0,), (0,)))
+        gram = dot(high, high, ((0,), (0,))) + (dot(low, low, ((0,), (0,))) + (cross + cross.T))
+        gram_ref[s] = jnp.where((row == 0) & (col == n - 1), square_ref[s], gram)
+
+
+def project(buffer, basis, squares, parts=4):
     slots, rows, cols = buffer.shape
     rank = basis.shape[-1]
-    part = rows // steps
     return pl.pallas_call(
         project_kernel,
-        grid=(slots, steps),
-        in_specs=[
-            pl.BlockSpec(memory_space=pltpu.SMEM),
-            pl.BlockSpec((1, part, cols), lambda s, i: (s, i, 0)),
-            pl.BlockSpec((1, cols, rank), lambda s, i: (s, 0, 0)),
-        ],
-        out_specs=[
-            pl.BlockSpec((1, part, rank), lambda s, i: (s, i, 0)),
-            pl.BlockSpec((1, rank, rank), lambda s, i: (s, 0, 0)),
-        ],
+        in_specs=[pl.BlockSpec(memory_space=pltpu.SMEM), HBM, VMEM],
+        out_specs=[VMEM, VMEM],
         out_shape=[
             jax.ShapeDtypeStruct((slots, rows, rank), F32),
             jax.ShapeDtypeStruct((slots, rank, rank), F32),
         ],
+        scratch_shapes=[pltpu.VMEM((slots, rows, cols), BF16), pltpu.SemaphoreType.DMA((slots, parts))],
         compiler_params=pltpu.CompilerParams(vmem_limit_bytes=24 << 20),
         name="project",
-    )(squares, buffer, basis)
+    )(squares, pltpu.with_memory_space_constraint(buffer, pltpu.HBM), basis)
 
 
 def eliminate(work_ref, slots, n):
     b = BLOCK
-    tiles = 2 * n // 128
+    tiles = n // 128
     sub = lax.broadcasted_iota(jnp.int32, (b, 128), 0)
+    sub_all = lax.broadcasted_iota(jnp.int32, (b, n), 0)
+    lane_all = lax.broadcasted_iota(jnp.int32, (b, n), 1)
     for j in range(n // b):
         lo, hi = j * b, (j + 1) * b
+        inside = (lane_all >= lo) & (lane_all < hi)
         panels = []
         cols = []
         for s in range(slots):
             panel = work_ref[s, lo:hi, :]
-            panels.append(panel)
             cols.append([jnp.broadcast_to(panel[:, lo + k : lo + k + 1], (b, 128)) for k in range(b)])
+            panels.append(jnp.where(inside, (lane_all - lo == sub_all).astype(F32), panel))
         for k in range(b):
             for s in range(slots):
                 c = cols[s]
@@ -105,9 +126,8 @@
                 p = panels[s]
                 pivot = p[k : k + 1] * jnp.concatenate([inv[:1]] * tiles, axis=1)
                 below_all = jnp.concatenate([below] * tiles, axis=1)
-                at_k = jnp.concatenate([sub == k] * tiles, axis=1)
-                pivot_all = jnp.broadcast_to(pivot, (b, 2 * n))
-                panels[s] = jnp.where(at_k, pivot_all, p - below_all * pivot_all)
+                pivot_all = jnp.broadcast_to(pivot, (b, n))
+                panels[s] = jnp.where(sub_all == k, pivot_all, p - below_all * pivot_all)
         for s in range(slots):
             work_ref[s, lo:hi, :] = panels[s]
             if hi < n:
@@ -115,13 +135,16 @@
                     panels[s][:, hi:n], panels[s], (((0,), (0,)), ((), ())),
                     precision=lax.Precision.HIGHEST, preferred_element_type=F32,
                 )
-                work_ref[s, hi:, :] = work_ref[s, hi:, :] - update
+                lane = lax.broadcasted_iota(jnp.int32, update.shape, 1)
+                old = jnp.where((lane >= lo) & (lane < hi), 0.0, work_ref[s, hi:, :])
+                work_ref[s, hi:, :] = old - update
 
 
 def factor_kernel(gram_ref, proj_ref, buffer_ref, ortho_ref, half_ref, blocks_ref, work_ref, block_ref, sum_ref, sems):
     slots, rows, n = proj_ref.shape
     cols = block_ref.shape[-1]
-    near_blocks, far, _, width, _ = blocks_ref.shape
+    far, width = blocks_ref.shape[1], blocks_ref.shape[3]
+    near = lax.axis_size(NEAR_Z)
     loads = [pltpu.make_async_copy(buffer_ref.at[s], block_ref.at[s], sems.at[s]) for s in range(slots)]
     for load in loads:
         load.start()
@@ -130,23 +153,19 @@
     for s in range(slots):
         gram = gram_ref[s * n : (s + 1) * n, :]
         mirror = jnp.broadcast_to(gram[n - 1 :, :1], (n, n))
-        work_ref[s, :, :n] = jnp.where((row == 0) & (col == n - 1), mirror, gram)
-        work_ref[s, :, n:] = (row == col).astype(F32)
+        work_ref[s] = jnp.where((row == 0) & (col == n - 1), mirror, gram)
     eliminate(work_ref, slots, n)
     for s in range(slots):
-        ortho = lax.dot_general(
-            proj_ref[s], work_ref[s, :, n:], (((1,), (1,)), ((), ())),
-            precision=lax.Precision.HIGHEST, preferred_element_type=F32,
-        )
+        high, low = halves(jnp.where(row >= col, work_ref[s], 0.0))
+        proj_high, proj_low = halves(proj_ref[s])
+        across = ((1,), (1,))
+        ortho = dot(proj_high, high, across) + (dot(proj_high, low, across) + dot(proj_low, high, across))
         ortho_ref[s] = ortho
-        half_ref[s] = ortho.astype(BF16)
+        half = ortho.astype(BF16)
+        half_ref[s] = half
         loads[s].wait()
-        half = half_ref[s]
         for c in range(0, cols, n):
-            sum_ref[c : c + n, :] = lax.dot_general(
-                block_ref[s, :, c : c + n], half, (((0,), (0,)), ((), ())), preferred_element_type=F32
-            )
-        near = lax.axis_size(NEAR_Z)
+            sum_ref[c : c + n, :] = dot(block_ref[s, :, c : c + n], half, ((0,), (0,)))
         for c in range(cols // width):
             x, z = divmod(c, far * near)
             f, m = divmod(z, near)
@@ -158,25 +177,24 @@
     cols = buffer.shape[-1]
     devices = lax.axis_size(SHARD)
     far = lax.axis_size(FAR_Z)
-    vmem = pl.BlockSpec(memory_space=pltpu.VMEM)
     return pl.pallas_call(
         factor_kernel,
-        in_specs=[vmem, vmem, pl.BlockSpec(memory_space=pl.ANY)],
-        out_specs=[vmem, vmem, vmem],
+        in_specs=[VMEM, VMEM, HBM],
+        out_specs=[VMEM, VMEM, VMEM],
         out_shape=[
             jax.ShapeDtypeStruct((slots, rows, rank), F32),
             jax.ShapeDtypeStruct((slots, rows, rank), BF16),
             jax.ShapeDtypeStruct((devices // far, far, slots, cols // devices, rank), BF16),
         ],
         scratch_shapes=[
-            pltpu.VMEM((slots, rank, 2 * rank), F32),
+            pltpu.VMEM((slots, rank, rank), F32),
             pltpu.VMEM((slots, rows, cols), BF16),
             pltpu.VMEM((cols, rank), F32),
             pltpu.SemaphoreType.DMA((slots,)),
         ],
         compiler_params=pltpu.CompilerParams(vmem_limit_bytes=32 << 20),
         name="factor",
-    )(gram, proj, buffer)
+    )(gram, proj, pltpu.with_memory_space_constraint(buffer, pltpu.HBM))
 
 
 def body(buffer, right_basis, layer_count):
@@ -202,6 +220,7 @@
     clip = jnp.minimum(1.0, CLIP_RMS * lax.rsqrt(jnp.maximum(totals[0] / totals[1], SQUARE_FLOOR)))
     left = jnp.where(keep, clip * math.sqrt(rows_all) * ortho, 0.0).astype(BF16)
 
+    right, left = lax.optimization_barrier((right, left))
     half_right = whole_rows(right.astype(BF16))
     colsq = jnp.sum(jnp.square(half_right.astype(F32)), axis=1, keepdims=True)
     right_step = jnp.where(keep, right * (math.sqrt(cols) * lax.rsqrt(colsq + 1.0)), 0.0)

time: 243 us -> 233 us (0.959)
  blocking collectives: 141 us -> 157 us
  waiting for transfers between devices: 35.2 us -> 23.5 us
  local copies, waits for them, and re-layouts: 11.9 us -> 3.88 us
  matrix products: 6.79 us -> 4.31 us
    all_to_all x6, blocking collectives: 131 us -> 147 us  [exchange(): return lax.all_to_all(blocks, axis, split_axis=0, concat_axis=0, tiled=True)]
    all_to_all x2, waiting for transfers between devices: 35.2 us -> 23.5 us  [exchange(): return lax.all_to_all(blocks, axis, split_axis=0, concat_axis=0, tiled=True)]
    unnamed x4, local copies, waits for them, and re-layouts: 5 us -> 0.02 us
    dot_general x1, matrix products: 6.79 us -> 4.31 us  [body(): jnp.einsum('kir,kjr->kij', half_left, half_right, preferred_element_type=...]
  transfers between devices with their start and end apart: 2 -> 2, of which waited for: 2 -> 1; matrix products, arithmetic and copies ran while one was open for 3% -> 3% of each run, Pallas kernels for 0% -> 0%
where the time goes in v4:
time: 233 us; the launch traced here: 232 us
  blocking collectives  157 us (67%)
  waiting for transfers between devices  23.5 us (10%)
  Pallas kernels  22.9 us (10%)
  other arithmetic  9.11 us (4%)
  starting transfers between devices  8.75 us (4%)
  matrix products  4.31 us (2%)
  local copies, waits for them, and re-layouts  3.88 us (2%)
  between operations  2.77 us (1%)
    all_to_all x6, blocking collectives, exchange(): return lax.all_to_all(blocks, axis, split_axis=0, concat_axis=0, tiled=True)  147 us
    all_to_all x2, waiting for transfers between devices, exchange(): return lax.all_to_all(blocks, axis, split_axis=0, concat_axis=0, tiled=True)  23.5 us
    pallas_call x1, Pallas kernels, factor(): pl.pallas_call(factor_kernel, in_specs=[VMEM, VMEM, HBM], out_specs=[VMEM...  16 us
    psum x1, blocking collectives, body(): totals = lax.psum(jnp.stack([squares, elements]), SEG)  10.6 us
    all_to_all x2, starting transfers between devices, exchange(): return lax.all_to_all(blocks, axis, split_axis=0, concat_axis=0, tiled=True)  8.75 us
    pallas_call x1, Pallas kernels, project(): pl.pallas_call(project_kernel, in_specs=[pl.BlockSpec(memory_space=pltpu....  6.99 us
  transfers between devices with their start and end apart: 2, of which 1 were waited for; matrix products, arithmetic and copies ran while one was open for 3% of the time, Pallas kernels for 0%

profile of v4, /device:TPU:24, one launch (start us, length us, event | category | flops | bytes accessed | tf_op | source)
XLA Modules:
  0.0 232.5 jit_solution(3359395315282274066)
XLA Ops:
  0.6 0.9 broadcast_in_dim.58
  1.5 20.3 %all_to_all.40 = bf16[4,2,72,256]{3,2,1,0:T(8,128)(2,1)S(1)} all-to-all(bf16[4,2,72,256]{3,2,1,0:T(8,128)(2,1)S(1)} %broadcast_in_dim.58), channel_id=1, replica_groups=mesh['segment_0'=4,'segment_1'=2,'x'=4,'z_far'=4,'z_near'=2] {'z_far'}, dimensions={0} | all-to-all | bytes 589824 | tf_op jit(solution)/shard_map/all_to_all | solution.py:27
  21.8 1.6 broadcast_in_dim.59
  23.4 4.8 %all-to-all-start.1 = ((bf16[8,4,2,72,256]{4,3,2,1,0:T(8,128)(2,1)}), bf16[8,4,2,72,256]{4,3,2,1,0:T(8,128)(2,1)S(1)}, u32[]{:S(2)}, u32[]{:S(2)}) async-start(bf16[8,4,2,72,256]{4,3,2,1,0:T(8,128)(2,1)} %broadcast_in_dim.59), calls=%async_computation.1 | async-start | bytes 4718592 | tf_op jit(solution)/shard_map/all_to_all | solution.py:27
  28.2 4.0 %fusion.square_ref = f32[2]{0:T(128)S(1)} fusion(bf16[2,576,2304]{2,1,0:T(8,128)(2,1)} %buffer_ref.3), kind=kLoop, calls=%fused_computation.2 | loop fusion | flops 7962622 | bytes 5308424 | tf_op jit(solution)/shard_map/reduce_sum | solution.py:210
  32.2 23.5 %all-to-all-done.1 = bf16[8,4,2,72,256]{4,3,2,1,0:T(8,128)(2,1)S(1)} async-done(((bf16[8,4,2,72,256]{4,3,2,1,0:T(8,128)(2,1)}), bf16[8,4,2,72,256]{4,3,2,1,0:T(8,128)(2,1)S(1)}, u32[]{:S(2)}, u32[]{:S(2)}) %all-to-all-start.1) | async-done | bytes 2359328 | tf_op jit(solution)/shard_map/all_to_all | solution.py:27
  55.7 0.2 copy.8
  55.9 7.0 %project.1 = (f32[2,576,256]{2,1,0:T(8,128)S(1)}, f32[2,256,256]{2,1,0:T(8,128)S(1)}) custom-call(f32[2]{0:T(128)S(1)} %fusion.square_ref, bf16[2,576,2304]{2,1,0:T(8,128)(2,1)} %buffer_ref.3, bf16[2,2304,256]{2,1,0:T(8,128)(2,1)S(1)} %bitcast.19), custom_call_target="tpu_custom_call" | custom-call | tf_op jit(solution)/shard_map/project/pallas_call | solution.py:89
  62.9 21.1 %all_to_all.41 = f32[32,16,256]{2,1,0:T(8,128)S(1)} all-to-all(f32[32,16,256]{2,1,0:T(8,128)S(1)} %bitcast.22), channel_id=1, replica_groups=mesh['segment_0'=4,'segment_1'=2,'x'=4,'z_far'=4,'z_near'=2] {'x','z_far..., dimensions={0} | all-to-all | bytes 1048576 | tf_op jit(solution)/shard_map/all_to_all | solution.py:27
  84.1 0.1 broadcast_in_dim.60
  84.1 22.1 %all_to_all.42 = f32[32,16,256]{2,1,0:T(8,128)S(1)} all-to-all(f32[32,16,256]{2,1,0:T(8,128)S(1)} %broadcast_in_dim.60), channel_id=1, replica_groups=mesh['segment_0'=4,'segment_1'=2,'x'=4,'z_far'=4,'z_near'=2] {'x','z_far..., dimensions={0} | all-to-all | bytes 1048576 | tf_op jit(solution)/shard_map/all_to_all | solution.py:27
  106.2 16.0 %factor.1 = (f32[2,576,256]{2,1,0:T(8,128)S(1)}, bf16[2,576,256]{2,1,0:T(8,128)(2,1)S(1)}, bf16[8,4,2,72,256]{4,3,2,1,0:T(8,128)(2,1)S(1)}) custom-call(f32[512,256]{1,0:T(8,128)S(1)} %bitcast.20, f32[2,576,256]{2,1,0:T(8,128)S(1)} %get-tuple-element.11.proj_ref, bf16[2,576,2304]{2,1,0:T(8,128)(2,1)} %buffer_ref.3), custom_call_target="tpu_custom_call" | custom-call | tf_op jit(solution)/shard_map/factor/pallas_call | solution.py:180
  122.1 32.8 %all_to_all.43 = bf16[8,4,2,72,256]{4,3,2,1,0:T(8,128)(2,1)S(1)} all-to-all(bf16[8,4,2,72,256]{4,3,2,1,0:T(8,128)(2,1)S(1)} %get-tuple-element.13), channel_id=1, replica_groups=mesh['segment_0'=4,'segment_1'=2,'x'=4,'z_far'=4,'z_near'=2] {'x','z_near'}, dimensions={0} | all-to-all | bytes 4718592 | tf_op jit(solution)/shard_map/all_to_all | solution.py:27
  154.9 1.1 convert_reduce_fusion
  156.0 4.0 %all-to-all-start.5 = ((f32[4,2,72,256]{3,2,1,0:T(8,128)}), f32[4,2,72,256]{3,2,1,0:T(8,128)S(1)}, u32[]{:S(2)}, u32[]{:S(2)}) async-start(f32[4,2,72,256]{3,2,1,0:T(8,128)} %convert_reduce_fusion), calls=%async_computation.5 | async-start | bytes 1179648 | tf_op jit(solution)/shard_map/all_to_all | solution.py:27
  160.6 0.1 slice.9
  160.7 0.1 reduce.1
  160.8 0.7 select_reduce_fusion
  161.5 0.8 pad_maximum_fusion
  162.3 10.6 %psum.7 = f32[2]{0:T(128)S(1)} all-reduce(f32[2]{0:T(128)S(1)} %pad_maximum_fusion), channel_id=1, replica_groups=mesh['segment_0'=4,'segment_1'=2,'x'=4,'z_far'=4,'z_near'=2] {'segment_0..., use_global_device_ids=true, to_apply=%region_5.6 | all-reduce | flops 2 | bytes 16 | tf_op jit(solution)/shard_map/psum | solution.py:219
  172.9 0.6 fusion.3
  174.8 1.0 select_convert_fusion
  175.9 0.0 all-to-all-done.5
  176.0 0.0 slice-start
  176.0 18.9 %all_to_all.44 = bf16[4,2,72,256]{3,2,1,0:T(8,128)(2,1)S(1)} all-to-all(bf16[4,2,72,256]{3,2,1,0:T(8,128)(2,1)S(1)} %broadcast_in_dim.64), channel_id=1, replica_groups=mesh['segment_0'=4,'segment_1'=2,'x'=4,'z_far'=4,'z_near'=2] {'z_far'}, dimensions={0} | all-to-all | bytes 589824 | tf_op jit(solution)/shard_map/all_to_all | solution.py:27
  194.9 0.2 broadcast_in_dim.65
  195.1 0.0 slice-start.1
  195.1 31.5 %all_to_all.45 = bf16[8,4,2,72,256]{4,3,2,1,0:T(8,128)(2,1)S(1)} all-to-all(bf16[8,4,2,72,256]{4,3,2,1,0:T(8,128)(2,1)S(1)} %broadcast_in_dim.65), channel_id=1, replica_groups=mesh['segment_0'=4,'segment_1'=2,'x'=4,'z_far'=4,'z_near'=2] {'x','z_near'}, dimensions={0} | all-to-all | bytes 4718592 | tf_op jit(solution)/shard_map/all_to_all | solution.py:27
  226.6 0.5 multiply_reduce_fusion
  227.2 0.2 copy.9
  227.4 0.7 multiply_select_fusion
  228.2 0.0 slice-done
  228.2 0.0 slice-done.1
  228.2 4.3 %fusion.2 = bf16[2,576,2304]{2,1,0:T(8,128)(2,1)} fusion(bf16[2,576,2304]{2,1,0:T(8,128)(2,1)S(1)} %bitcast.24, bf16[2,576,256]{2,1,0:T(8,128)(2,1)S(1)} %get-tuple-element.12, bf16[2,2304,256]{2,1,0:T(8,128)(2,1)S(1)} %bitcast.28, pred[2]{0:T(512)(128)(4,1)S(1)} %iota_compare_fusion), kind=kOutput, calls=%fused_computation.4 | convolution fusion | flops 1372225536 | bytes 13565954 | tf_op jit(solution)/shard_map/kir,kjr->kij/dot_general | solution.py:228
  (7 shorter events, 0.1 us)
Async XLA Ops:
  23.4 32.3 %all-to-all-start.1 = ((bf16[8,4,2,72,256]{4,3,2,1,0:T(8,128)(2,1)}), bf16[8,4,2,72,256]{4,3,2,1,0:T(8,128)(2,1)S(1)}, u32[]{:S(2)}, u32[]{:S(2)}) async-start(bf16[8,4,2,72,256]{4,3,2,1,0:T(8,128)(2,1)} %broadcast_in_dim.59), calls=%async_computation.1 | async-start | bytes 4718592 | tf_op jit(solution)/shard_map/all_to_all | solution.py:27
  156.0 19.9 %all-to-all-start.5 = ((f32[4,2,72,256]{3,2,1,0:T(8,128)}), f32[4,2,72,256]{3,2,1,0:T(8,128)S(1)}, u32[]{:S(2)}, u32[]{:S(2)}) async-start(f32[4,2,72,256]{3,2,1,0:T(8,128)} %convert_reduce_fusion), calls=%async_computation.5 | async-start | bytes 1179648 | tf_op jit(solution)/shard_map/all_to_all | solution.py:27
  176.0 52.2 %slice-start = ((s8[5308416]{0:T(1024)(128)(4,1)}), s8[4194304]{0:T(1024)(128)(4,1)S(1)}, s32[]{:S(2)}) async-start(s8[5308416]{0:T(1024)(128)(4,1)} %bitcast.23), calls=%async_computation.8 | async-start | bytes 8388608
  195.1 33.1 %slice-start.1 = ((s8[5308416]{0:T(1024)(128)(4,1)}), s8[1114112]{0:T(1024)(128)(4,1)S(1)}, s32[]{:S(2)}) async-start(s8[5308416]{0:T(1024)(128)(4,1)} %bitcast.23), calls=%async_computation.9 | async-start | bytes 2228224

commit v5 on v4

--- a/solution.py
+++ b/solution.py
@@ -1,3 +1,4 @@
+import functools
 import math
 
 import jax
@@ -38,11 +39,6 @@
     return plane.transpose(3, 0, 2, 1, 4, 5).reshape(slots, -1, rank)
 
 
-def summed_rows(blocks):
-    line = exchange(blocks, PLANE).astype(F32).sum(axis=0)
-    return exchange(line, FAR_Z).sum(axis=0)
-
-
 def halves(value):
     high = value.astype(BF16)
     return high, (value - high.astype(F32)).astype(BF16)
@@ -58,7 +54,7 @@
 HBM = pl.BlockSpec(memory_space=pltpu.HBM)
 
 
-def project_kernel(square_ref, buffer_ref, basis_ref, proj_ref, gram_ref, block_ref, sems):
+def project_kernel(square_ref, buffer_ref, basis_ref, proj_ref, pack_ref, block_ref, sems):
     slots, rows, n = proj_ref.shape
     parts = sems.shape[1]
     part = rows // parts
@@ -72,6 +68,7 @@
             load(s, i).start()
     row = lax.broadcasted_iota(jnp.int32, (n, n), 0)
     col = lax.broadcasted_iota(jnp.int32, (n, n), 1)
+    grams = []
     for s in range(slots):
         for i in range(parts):
             load(s, i).wait()
@@ -79,8 +76,13 @@
             proj_ref[s, lines, :] = jnp.dot(block_ref[s, lines, :], basis_ref[s], preferred_element_type=F32)
         high, low = halves(proj_ref[s])
         cross = dot(high, low, ((0,), (0,)))
-        gram = dot(high, high, ((0,), (0,))) + (dot(low, low, ((0,), (0,))) + (cross + cross.T))
-        gram_ref[s] = jnp.where((row == 0) & (col == n - 1), square_ref[s], gram)
+        grams.append(dot(high, high, ((0,), (0,))) + (dot(low, low, ((0,), (0,))) + (cross + cross.T)))
+    lower, upper = grams
+    pack_ref[:, :n] = jnp.where(row >= col, lower, upper)
+    diagonal = jnp.sum(jnp.where(row == col, upper, 0.0), axis=1, keepdims=True)
+    row, col = row[:, :128], col[:, :128]
+    squares = jnp.where(row == 0, square_ref[0], square_ref[1])
+    pack_ref[:, n:] = jnp.where(col == 0, diagonal, jnp.where((col == 1) & (row < slots), squares, 0.0))
 
 
 def project(buffer, basis, squares, parts=4):
@@ -92,7 +94,7 @@
         out_specs=[VMEM, VMEM],
         out_shape=[
             jax.ShapeDtypeStruct((slots, rows, rank), F32),
-            jax.ShapeDtypeStruct((slots, rank, rank), F32),
+            jax.ShapeDtypeStruct((rank, rank + 128), F32),
         ],
         scratch_shapes=[pltpu.VMEM((slots, rows, cols), BF16), pltpu.SemaphoreType.DMA((slots, parts))],
         compiler_params=pltpu.CompilerParams(vmem_limit_bytes=24 << 20),
@@ -140,20 +142,20 @@
                 work_ref[s, hi:, :] = old - update
 
 
-def factor_kernel(gram_ref, proj_ref, buffer_ref, ortho_ref, half_ref, blocks_ref, work_ref, block_ref, sum_ref, sems):
+def factor_kernel(near, pack_ref, proj_ref, buffer_ref, ortho_ref, half_ref, blocks_ref, work_ref, block_ref, sum_ref, sems):
     slots, rows, n = proj_ref.shape
     cols = block_ref.shape[-1]
     far, width = blocks_ref.shape[1], blocks_ref.shape[3]
-    near = lax.axis_size(NEAR_Z)
     loads = [pltpu.make_async_copy(buffer_ref.at[s], block_ref.at[s], sems.at[s]) for s in range(slots)]
     for load in loads:
         load.start()
     row = lax.broadcasted_iota(jnp.int32, (n, n), 0)
     col = lax.broadcasted_iota(jnp.int32, (n, n), 1)
-    for s in range(slots):
-        gram = gram_ref[s * n : (s + 1) * n, :]
-        mirror = jnp.broadcast_to(gram[n - 1 :, :1], (n, n))
-        work_ref[s] = jnp.where((row == 0) & (col == n - 1), mirror, gram)
+    pack = pack_ref[:, :n]
+    turned = pack.T
+    work_ref[0] = jnp.where(row >= col, pack, turned)
+    diagonal = jnp.broadcast_to(pack_ref[:, n : n + 1], (n, n))
+    work_ref[1] = jnp.where(row < col, pack, jnp.where(row > col, turned, diagonal))
     eliminate(work_ref, slots, n)
     for s in range(slots):
         high, low = halves(jnp.where(row >= col, work_ref[s], 0.0))
@@ -172,13 +174,11 @@
             blocks_ref[x * near + m, f, s] = sum_ref[c * width : (c + 1) * width, :].astype(BF16)
 
 
-def factor(gram, proj, buffer):
+def factor(pack, proj, buffer, far, near, devices):
     slots, rows, rank = proj.shape
     cols = buffer.shape[-1]
-    devices = lax.axis_size(SHARD)
-    far = lax.axis_size(FAR_Z)
     return pl.pallas_call(
-        factor_kernel,
+        functools.partial(factor_kernel, near),
         in_specs=[VMEM, VMEM, HBM],
         out_specs=[VMEM, VMEM, VMEM],
         out_shape=[
@@ -194,7 +194,26 @@
         ],
         compiler_params=pltpu.CompilerParams(vmem_limit_bytes=32 << 20),
         name="factor",
-    )(gram, proj, pltpu.with_memory_space_constraint(buffer, pltpu.HBM))
+    )(pack, proj, pltpu.with_memory_space_constraint(buffer, pltpu.HBM))
+
+
+def add_kernel(blocks_ref, out_ref):
+    for i in range(blocks_ref.shape[1]):
+        total = blocks_ref[0, i].astype(F32)
+        for j in range(1, blocks_ref.shape[0]):
+            total = total + blocks_ref[j, i].astype(F32)
+        out_ref[i] = total.astype(BF16)
+
+
+def added(blocks):
+    return pl.pallas_call(
+        add_kernel,
+        in_specs=[VMEM],
+        out_specs=VMEM,
+        out_shape=jax.ShapeDtypeStruct(blocks.shape[1:], BF16),
+        compiler_params=pltpu.CompilerParams(vmem_limit_bytes=12 << 20),
+        name="added",
+    )(blocks)
 
 
 def body(buffer, right_basis, layer_count):
@@ -208,19 +227,21 @@
 
     basis = whole_rows(right_basis)
     per_slot = jnp.sum(jnp.square(buffer.astype(F32)), axis=(1, 2))
-    proj, gram = project(buffer, basis, per_slot)
-    part = exchange(gram.reshape(devices, -1, rank), SHARD).sum(axis=0)
-    gram = spread(part, SHARD).reshape(slots * rank, rank)
-    ortho, half_left, blocks = factor(gram, proj, buffer)
-    right = summed_rows(blocks)
-
-    squares = jnp.sum(jnp.where(used, gram[::rank, rank - 1], 0.0))
+    proj, pack = project(buffer, basis, per_slot)
+    part = exchange(pack.reshape(devices, -1, pack.shape[-1]), SHARD).sum(axis=0)
+    pack = spread(part, SHARD).reshape(pack.shape)
+    sizes = lax.axis_size(FAR_Z), lax.axis_size(NEAR_Z), devices
+    ortho, half_left, blocks = factor(pack, proj, buffer, *sizes)
+    line = added(exchange(blocks, PLANE))
+
+    squares = jnp.sum(jnp.where(used, pack[:slots, rank + 1], 0.0))
     elements = count.astype(F32) * float(rows_all * cols)
     totals = lax.psum(jnp.stack([squares, elements]), SEG)
     clip = jnp.minimum(1.0, CLIP_RMS * lax.rsqrt(jnp.maximum(totals[0] / totals[1], SQUARE_FLOOR)))
     left = jnp.where(keep, clip * math.sqrt(rows_all) * ortho, 0.0).astype(BF16)
 
-    right, left = lax.optimization_barrier((right, left))
+    line, left = lax.optimization_barrier((line, left))
+    right = exchange(line, FAR_Z).astype(F32).sum(axis=0)
     half_right = whole_rows(right.astype(BF16))
     colsq = jnp.sum(jnp.square(half_right.astype(F32)), axis=1, keepdims=True)
     right_step = jnp.where(keep, right * (math.sqrt(cols) * lax.rsqrt(colsq + 1.0)), 0.0)

time: 233 us -> 217 us (0.931)
  blocking collectives: 157 us -> 127 us
  waiting for transfers between devices: 23.5 us -> 35 us
  local copies, waits for them, and re-layouts: 3.88 us -> 6.35 us
    all_to_all x6, blocking collectives: 147 us -> 116 us  [exchange(): return lax.all_to_all(blocks, axis, split_axis=0, concat_axis=0, tiled=True)]
    all_to_all x2, waiting for transfers between devices: 23.5 us -> 35 us  [exchange(): return lax.all_to_all(blocks, axis, split_axis=0, concat_axis=0, tiled=True)]
    unnamed x4 -> x8, local copies, waits for them, and re-layouts: 0.02 us -> 2.42 us
    pallas_call x1 -> x2, Pallas kernels: 16 us -> 15.7 us  [the longest x1 15.4 us: factor(): pl.pallas_call(functools.partial(factor_kernel, near), in_specs=[VMEM, VM...]
  transfers between devices with their start and end apart: 2 -> 2, of which waited for: 1 -> 2; matrix products, arithmetic and copies ran while one was open for 3% -> 4% of each run, Pallas kernels for 0% -> 0%
where the time goes in v5:
time: 217 us; the launch traced here: 216 us
  blocking collectives  127 us (59%)
  waiting for transfers between devices  35 us (16%)
  Pallas kernels  22.8 us (11%)
  starting transfers between devices  9.09 us (4%)
  other arithmetic  9.04 us (4%)
  local copies, waits for them, and re-layouts  6.35 us (3%)
  matrix products  4.31 us (2%)
  between operations  2.78 us (1%)
    all_to_all x6, blocking collectives, exchange(): return lax.all_to_all(blocks, axis, split_axis=0, concat_axis=0, tiled=True)  116 us
    all_to_all x2, waiting for transfers between devices, exchange(): return lax.all_to_all(blocks, axis, split_axis=0, concat_axis=0, tiled=True)  35 us
    pallas_call x1, Pallas kernels, factor(): pl.pallas_call(functools.partial(factor_kernel, near), in_specs=[VMEM, VM...  15.4 us
    psum x1, blocking collectives, body(): totals = lax.psum(jnp.stack([squares, elements]), SEG)  10.6 us
    all_to_all x2, starting transfers between devices, exchange(): return lax.all_to_all(blocks, axis, split_axis=0, concat_axis=0, tiled=True)  9.09 us
    pallas_call x1, Pallas kernels, project(): pl.pallas_call(project_kernel, in_specs=[pl.BlockSpec(memory_space=pltpu....  7.07 us
  transfers between devices with their start and end apart: 2, of which 2 were waited for; matrix products, arithmetic and copies ran while one was open for 4% of the time, Pallas kernels for 0%

profile of v5, /device:TPU:24, one launch (start us, length us, event | category | flops | bytes accessed | tf_op | source)
XLA Modules:
  0.0 216.4 jit_solution(6283407788063082812)
XLA Ops:
  0.6 0.9 broadcast_in_dim.58
  1.5 20.3 %all_to_all.40 = bf16[4,2,72,256]{3,2,1,0:T(8,128)(2,1)S(1)} all-to-all(bf16[4,2,72,256]{3,2,1,0:T(8,128)(2,1)S(1)} %broadcast_in_dim.58), channel_id=1, replica_groups=mesh['segment_0'=4,'segment_1'=2,'x'=4,'z_far'=4,'z_near'=2] {'z_far'}, dimensions={0} | all-to-all | bytes 589824 | tf_op jit(solution)/shard_map/all_to_all | solution.py:28
  21.8 1.6 broadcast_in_dim.59
  23.4 4.8 %all-to-all-start.1 = ((bf16[8,4,2,72,256]{4,3,2,1,0:T(8,128)(2,1)}), bf16[8,4,2,72,256]{4,3,2,1,0:T(8,128)(2,1)S(1)}, u32[]{:S(2)}, u32[]{:S(2)}) async-start(bf16[8,4,2,72,256]{4,3,2,1,0:T(8,128)(2,1)} %broadcast_in_dim.59), calls=%async_computation.1 | async-start | bytes 4718592 | tf_op jit(solution)/shard_map/all_to_all | solution.py:28
  28.2 4.0 %fusion.square_ref = f32[2]{0:T(128)S(1)} fusion(bf16[2,576,2304]{2,1,0:T(8,128)(2,1)} %buffer_ref.3), kind=kLoop, calls=%fused_computation.2 | loop fusion | flops 7962622 | bytes 5308424 | tf_op jit(solution)/shard_map/reduce_sum | solution.py:229
  32.2 23.5 %all-to-all-done.1 = bf16[8,4,2,72,256]{4,3,2,1,0:T(8,128)(2,1)S(1)} async-done(((bf16[8,4,2,72,256]{4,3,2,1,0:T(8,128)(2,1)}), bf16[8,4,2,72,256]{4,3,2,1,0:T(8,128)(2,1)S(1)}, u32[]{:S(2)}, u32[]{:S(2)}) %all-to-all-start.1) | async-done | bytes 2359328 | tf_op jit(solution)/shard_map/all_to_all | solution.py:28
  55.7 0.2 copy.6
  55.9 7.1 %project.1 = (f32[2,576,256]{2,1,0:T(8,128)S(1)}, f32[256,384]{1,0:T(8,128)S(1)}) custom-call(f32[2]{0:T(128)S(1)} %fusion.square_ref, bf16[2,576,2304]{2,1,0:T(8,128)(2,1)} %buffer_ref.3, bf16[2,2304,256]{2,1,0:T(8,128)(2,1)S(1)} %bitcast.19), custom_call_target="tpu_custom_call" | custom-call | tf_op jit(solution)/shard_map/project/pallas_call | solution.py:91
  63.0 18.7 %all_to_all.41 = f32[32,8,384]{2,1,0:T(8,128)S(1)} all-to-all(f32[32,8,384]{2,1,0:T(8,128)S(1)} %bitcast.22), channel_id=1, replica_groups=mesh['segment_0'=4,'segment_1'=2,'x'=4,'z_far'=4,'z_near'=2] {'x','z_far..., dimensions={0} | all-to-all | bytes 786432 | tf_op jit(solution)/shard_map/all_to_all | solution.py:28
  81.7 19.4 %all_to_all.42 = f32[32,8,384]{2,1,0:T(8,128)S(1)} all-to-all(f32[32,8,384]{2,1,0:T(8,128)S(1)} %broadcast_in_dim.60), channel_id=1, replica_groups=mesh['segment_0'=4,'segment_1'=2,'x'=4,'z_far'=4,'z_near'=2] {'x','z_far..., dimensions={0} | all-to-all | bytes 786432 | tf_op jit(solution)/shard_map/all_to_all | solution.py:28
  101.2 15.4 %factor.1 = (f32[2,576,256]{2,1,0:T(8,128)S(1)}, bf16[2,576,256]{2,1,0:T(8,128)(2,1)S(1)}, bf16[8,4,2,72,256]{4,3,2,1,0:T(8,128)(2,1)S(1)}) custom-call(f32[256,384]{1,0:T(8,128)S(1)} %bitcast.20, f32[2,576,256]{2,1,0:T(8,128)S(1)} %get-tuple-element.11.proj_ref, bf16[2,576,2304]{2,1,0:T(8,128)(2,1)} %buffer_ref.3), custom_call_target="tpu_custom_call" | custom-call | tf_op jit(solution)/shard_map/factor/pallas_call | solution.py:180
  116.6 0.0 copy-start
  116.6 1.4 copy-done
  118.0 0.0 copy-start.1
  118.0 1.0 copy-done.1
  119.0 4.3 %all-to-all-start.4 = ((bf16[8,4,2,72,256]{4,3,2,1,0:T(8,128)(2,1)}), bf16[8,4,2,72,256]{4,3,2,1,0:T(8,128)(2,1)S(1)}, u32[]{:S(2)}, u32[]{:S(2)}) async-start(bf16[8,4,2,72,256]{4,3,2,1,0:T(8,128)(2,1)} %copy-done), calls=%async_computation.4 | async-start | bytes 4718592 | tf_op jit(solution)/shard_map/all_to_all | solution.py:28
  123.9 0.2 slice_reduce_fusion
  124.1 0.7 select_reduce_fusion
  124.8 0.7 pad_maximum_fusion
  125.5 10.6 %psum.7 = f32[2]{0:T(128)S(1)} all-reduce(f32[2]{0:T(128)S(1)} %pad_maximum_fusion), channel_id=1, replica_groups=mesh['segment_0'=4,'segment_1'=2,'x'=4,'z_far'=4,'z_near'=2] {'segment_0..., use_global_device_ids=true, to_apply=%region_3.4 | all-reduce | flops 2 | bytes 16 | tf_op jit(solution)/shard_map/psum | solution.py:239
  136.1 0.6 fusion.3
  138.0 2.3 %select_convert_fusion = bf16[2,576,256]{2,1,0:T(8,128)(2,1)} fusion(f32[2,576,256]{2,1,0:T(8,128)} %copy-done.1, f32[]{:T(128)} %bitcast.8, pred[2]{0:T(512)(128)(4,1)S(1)} %iota_compare_fusion), kind=kLoop, calls=%fused_computation.6 | loop fusion | flops 884736 | bytes 1769478 | tf_op jit(solution)/shard_map/convert_element_type | solution.py:241
  140.3 11.5 %all-to-all-done.4.blocks_ref = bf16[8,4,2,72,256]{4,3,2,1,0:T(8,128)(2,1)S(1)} async-done(((bf16[8,4,2,72,256]{4,3,2,1,0:T(8,128)(2,1)}), bf16[8,4,2,72,256]{4,3,2,1,0:T(8,128)(2,1)S(1)}, u32[]{:S(2)}, u32[]{:S(2)}) %all-to-all-start.4) | async-done | bytes 2359328 | tf_op jit(solution)/shard_map/all_to_all | solution.py:28
  151.9 0.3 added.1
  152.2 13.2 %all_to_all.43 = bf16[4,2,72,256]{3,2,1,0:T(8,128)(2,1)S(1)} all-to-all(bf16[4,2,72,256]{3,2,1,0:T(8,128)(2,1)S(1)} %added.1), channel_id=1, replica_groups=mesh['segment_0'=4,'segment_1'=2,'x'=4,'z_far'=4,'z_near'=2] {'z_far'}, dimensions={0} | all-to-all | bytes 589824 | tf_op jit(solution)/shard_map/all_to_all | solution.py:28
  165.4 0.0 slice-start
  165.5 12.8 %all_to_all.44 = bf16[4,2,72,256]{3,2,1,0:T(8,128)(2,1)S(1)} all-to-all(bf16[4,2,72,256]{3,2,1,0:T(8,128)(2,1)S(1)} %broadcast_in_dim.64), channel_id=1, replica_groups=mesh['segment_0'=4,'segment_1'=2,'x'=4,'z_far'=4,'z_near'=2] {'z_far'}, dimensions={0} | all-to-all | bytes 589824 | tf_op jit(solution)/shard_map/all_to_all | solution.py:28
  178.2 0.2 broadcast_in_dim.65
  178.4 0.0 slice-start.1
  178.5 32.1 %all_to_all.45 = bf16[8,4,2,72,256]{4,3,2,1,0:T(8,128)(2,1)S(1)} all-to-all(bf16[8,4,2,72,256]{4,3,2,1,0:T(8,128)(2,1)S(1)} %broadcast_in_dim.65), channel_id=1, replica_groups=mesh['segment_0'=4,'segment_1'=2,'x'=4,'z_far'=4,'z_near'=2] {'x','z_near'}, dimensions={0} | all-to-all | bytes 4718592 | tf_op jit(solution)/shard_map/all_to_all | solution.py:28
  210.6 0.5 multiply_reduce_fusion
  211.1 0.2 copy.7
  211.4 0.7 multiply_select_fusion
  212.1 0.0 slice-done
  212.1 0.0 slice-done.1
  212.1 4.3 %fusion.2 = bf16[2,576,2304]{2,1,0:T(8,128)(2,1)} fusion(bf16[2,576,2304]{2,1,0:T(8,128)(2,1)S(1)} %bitcast.24, bf16[2,576,256]{2,1,0:T(8,128)(2,1)S(1)} %get-tuple-element.12, bf16[2,2304,256]{2,1,0:T(8,128)(2,1)S(1)} %bitcast.28, pred[2]{0:T(512)(128)(4,1)S(1)} %iota_compare_fusion), kind=kOutput, calls=%fused_computation.4 | convolution fusion | flops 1372225536 | bytes 13565954 | tf_op jit(solution)/shard_map/kir,kjr->kij/dot_general | solution.py:249
  (8 shorter events, 0.1 us)
Async XLA Ops:
  23.4 32.3 %all-to-all-start.1 = ((bf16[8,4,2,72,256]{4,3,2,1,0:T(8,128)(2,1)}), bf16[8,4,2,72,256]{4,3,2,1,0:T(8,128)(2,1)S(1)}, u32[]{:S(2)}, u32[]{:S(2)}) async-start(bf16[8,4,2,72,256]{4,3,2,1,0:T(8,128)(2,1)} %broadcast_in_dim.59), calls=%async_computation.1 | async-start | bytes 4718592 | tf_op jit(solution)/shard_map/all_to_all | solution.py:28
  116.6 1.4 copy-start
  118.0 1.0 copy-start.1
  119.0 32.9 %all-to-all-start.4 = ((bf16[8,4,2,72,256]{4,3,2,1,0:T(8,128)(2,1)}), bf16[8,4,2,72,256]{4,3,2,1,0:T(8,128)(2,1)S(1)}, u32[]{:S(2)}, u32[]{:S(2)}) async-start(bf16[8,4,2,72,256]{4,3,2,1,0:T(8,128)(2,1)} %copy-done), calls=%async_computation.4 | async-start | bytes 4718592 | tf_op jit(solution)/shard_map/all_to_all | solution.py:28
  165.4 46.7 %slice-start = ((s8[5308416]{0:T(1024)(128)(4,1)}), s8[4194304]{0:T(1024)(128)(4,1)S(1)}, s32[]{:S(2)}) async-start(s8[5308416]{0:T(1024)(128)(4,1)} %bitcast.23), calls=%async_computation.8 | async-start | bytes 8388608
  178.4 33.7 %slice-start.1 = ((s8[5308416]{0:T(1024)(128)(4,1)}), s8[1114112]{0:T(1024)(128)(4,1)S(1)}, s32[]{:S(2)}) async-start(s8[5308416]{0:T(1024)(128)(4,1)} %bitcast.23), calls=%async_computation.9 | async-start | bytes 2228224

commit v6 on v5

--- a/solution.py
+++ b/solution.py
@@ -51,29 +51,12 @@
 VMEM = pl.BlockSpec(memory_space=pltpu.VMEM)
 
 
-HBM = pl.BlockSpec(memory_space=pltpu.HBM)
-
-
-def project_kernel(square_ref, buffer_ref, basis_ref, proj_ref, pack_ref, block_ref, sems):
+def pack_kernel(total_ref, proj_ref, pack_ref):
     slots, rows, n = proj_ref.shape
-    parts = sems.shape[1]
-    part = rows // parts
-
-    def load(s, i):
-        at = pl.ds(i * part, part)
-        return pltpu.make_async_copy(buffer_ref.at[s, at], block_ref.at[s, at], sems.at[s, i])
-
-    for s in range(slots):
-        for i in range(parts):
-            load(s, i).start()
     row = lax.broadcasted_iota(jnp.int32, (n, n), 0)
     col = lax.broadcasted_iota(jnp.int32, (n, n), 1)
     grams = []
     for s in range(slots):
-        for i in range(parts):
-            load(s, i).wait()
-            lines = slice(i * part, (i + 1) * part)
-            proj_ref[s, lines, :] = jnp.dot(block_ref[s, lines, :], basis_ref[s], preferred_element_type=F32)
         high, low = halves(proj_ref[s])
         cross = dot(high, low, ((0,), (0,)))
         grams.append(dot(high, high, ((0,), (0,))) + (dot(low, low, ((0,), (0,))) + (cross + cross.T)))
@@ -81,25 +64,23 @@
     pack_ref[:, :n] = jnp.where(row >= col, lower, upper)
     diagonal = jnp.sum(jnp.where(row == col, upper, 0.0), axis=1, keepdims=True)
     row, col = row[:, :128], col[:, :128]
-    squares = jnp.where(row == 0, square_ref[0], square_ref[1])
-    pack_ref[:, n:] = jnp.where(col == 0, diagonal, jnp.where((col == 1) & (row < slots), squares, 0.0))
-
-
-def project(buffer, basis, squares, parts=4):
-    slots, rows, cols = buffer.shape
-    rank = basis.shape[-1]
+    totals = jnp.where(row == 0, total_ref[0], total_ref[1])
+    pack_ref[:, n:] = jnp.where(col == 0, diagonal, jnp.where((col == 1) & (row < 2), totals, 0.0))
+
+
+def packed_grams(proj, totals):
+    rank = proj.shape[-1]
     return pl.pallas_call(
-        project_kernel,
-        in_specs=[pl.BlockSpec(memory_space=pltpu.SMEM), HBM, VMEM],
-        out_specs=[VMEM, VMEM],
-        out_shape=[
-            jax.ShapeDtypeStruct((slots, rows, rank), F32),
-            jax.ShapeDtypeStruct((rank, rank + 128), F32),
-        ],
-        scratch_shapes=[pltpu.VMEM((slots, rows, cols), BF16), pltpu.SemaphoreType.DMA((slots, parts))],
-        compiler_params=pltpu.CompilerParams(vmem_limit_bytes=24 << 20),
-        name="project",
-    )(squares, pltpu.with_memory_space_constraint(buffer, pltpu.HBM), basis)
+        pack_kernel,
+        in_specs=[pl.BlockSpec(memory_space=pltpu.SMEM), VMEM],
+        out_specs=VMEM,
+        out_shape=jax.ShapeDtypeStruct((rank, rank + 128), F32),
+        compiler_params=pltpu.CompilerParams(vmem_limit_bytes=12 << 20),
+        name="packed_grams",
+    )(totals, proj)
+
+
+HBM = pl.BlockSpec(memory_space=pltpu.HBM)
 
 
 def eliminate(work_ref, slots, n):
@@ -132,17 +113,18 @@
                 panels[s] = jnp.where(sub_all == k, pivot_all, p - below_all * pivot_all)
         for s in range(slots):
             work_ref[s, lo:hi, :] = panels[s]
-            if hi < n:
-                update = lax.dot_general(
-                    panels[s][:, hi:n], panels[s], (((0,), (0,)), ((), ())),
-                    precision=lax.Precision.HIGHEST, preferred_element_type=F32,
-                )
-                lane = lax.broadcasted_iota(jnp.int32, update.shape, 1)
-                old = jnp.where((lane >= lo) & (lane < hi), 0.0, work_ref[s, hi:, :])
-                work_ref[s, hi:, :] = old - update
-
-
-def factor_kernel(near, pack_ref, proj_ref, buffer_ref, ortho_ref, half_ref, blocks_ref, work_ref, block_ref, sum_ref, sems):
+            for f, g in ((hi, min(hi + b, n)), (hi + b, n)):
+                if f < g:
+                    update = lax.dot_general(
+                        panels[s][:, f:g], panels[s], (((0,), (0,)), ((), ())),
+                        precision=lax.Precision.HIGHEST, preferred_element_type=F32,
+                    )
+                    lane = lax.broadcasted_iota(jnp.int32, update.shape, 1)
+                    old = jnp.where((lane >= lo) & (lane < hi), 0.0, work_ref[s, f:g, :])
+                    work_ref[s, f:g, :] = old - update
+
+
+def factor_kernel(near, scale, count_ref, pack_ref, proj_ref, buffer_ref, left_ref, half_ref, blocks_ref, work_ref, block_ref, sum_ref, sems):
     slots, rows, n = proj_ref.shape
     cols = block_ref.shape[-1]
     far, width = blocks_ref.shape[1], blocks_ref.shape[3]
@@ -151,6 +133,9 @@
         load.start()
     row = lax.broadcasted_iota(jnp.int32, (n, n), 0)
     col = lax.broadcasted_iota(jnp.int32, (n, n), 1)
+    squares, elements = pack_ref[:1, n + 1 : n + 2], pack_ref[1:2, n + 1 : n + 2]
+    clip = jnp.minimum(1.0, CLIP_RMS * lax.rsqrt(jnp.maximum(squares / elements, SQUARE_FLOOR)))
+    size = jnp.broadcast_to(clip * scale, (rows, n))
     pack = pack_ref[:, :n]
     turned = pack.T
     work_ref[0] = jnp.where(row >= col, pack, turned)
@@ -162,7 +147,7 @@
         proj_high, proj_low = halves(proj_ref[s])
         across = ((1,), (1,))
         ortho = dot(proj_high, high, across) + (dot(proj_high, low, across) + dot(proj_low, high, across))
-        ortho_ref[s] = ortho
+        left_ref[s] = jnp.where(count_ref[0] > s, size * ortho, 0.0).astype(BF16)
         half = ortho.astype(BF16)
         half_ref[s] = half
         loads[s].wait()
@@ -174,15 +159,15 @@
             blocks_ref[x * near + m, f, s] = sum_ref[c * width : (c + 1) * width, :].astype(BF16)
 
 
-def factor(pack, proj, buffer, far, near, devices):
+def factor(count, pack, proj, buffer, far, near, devices):
     slots, rows, rank = proj.shape
     cols = buffer.shape[-1]
     return pl.pallas_call(
-        functools.partial(factor_kernel, near),
-        in_specs=[VMEM, VMEM, HBM],
+        functools.partial(factor_kernel, near, math.sqrt(rows * devices)),
+        in_specs=[pl.BlockSpec(memory_space=pltpu.SMEM), VMEM, VMEM, HBM],
         out_specs=[VMEM, VMEM, VMEM],
         out_shape=[
-            jax.ShapeDtypeStruct((slots, rows, rank), F32),
+            jax.ShapeDtypeStruct((slots, rows, rank), BF16),
             jax.ShapeDtypeStruct((slots, rows, rank), BF16),
             jax.ShapeDtypeStruct((devices // far, far, slots, cols // devices, rank), BF16),
         ],
@@ -194,7 +179,7 @@
         ],
         compiler_params=pltpu.CompilerParams(vmem_limit_bytes=32 << 20),
         name="factor",
-    )(pack, proj, pltpu.with_memory_space_constraint(buffer, pltpu.HBM))
+    )(count, pack, proj, pltpu.with_memory_space_constraint(buffer, pltpu.HBM))
 
 
 def add_kernel(blocks_ref, out_ref):
@@ -220,28 +205,24 @@
     slots, rows_dev, cols = buffer.shape
     rank = right_basis.shape[-1]
     devices = lax.axis_size(SHARD)
-    rows_all = rows_dev * devices
     count = layer_count[0]
     used = jnp.arange(slots, dtype=jnp.int32) < count
     keep = used[:, None, None]
 
     basis = whole_rows(right_basis)
-    per_slot = jnp.sum(jnp.square(buffer.astype(F32)), axis=(1, 2))
-    proj, pack = project(buffer, basis, per_slot)
+    squares = jnp.sum(jnp.square(buffer.astype(F32)), axis=(1, 2))
+    squares = jnp.sum(jnp.where(used, squares, 0.0))
+    elements = count.astype(F32) * float(rows_dev * cols)
+    totals = lax.psum(jnp.stack([squares, elements]), SEG)
+    proj = jnp.einsum("kij,kjr->kir", buffer, basis, preferred_element_type=F32)
+    pack = packed_grams(proj, totals)
     part = exchange(pack.reshape(devices, -1, pack.shape[-1]), SHARD).sum(axis=0)
     pack = spread(part, SHARD).reshape(pack.shape)
     sizes = lax.axis_size(FAR_Z), lax.axis_size(NEAR_Z), devices
-    ortho, half_left, blocks = factor(pack, proj, buffer, *sizes)
+    left, half_left, blocks = factor(layer_count, pack, proj, buffer, *sizes)
     line = added(exchange(blocks, PLANE))
-
-    squares = jnp.sum(jnp.where(used, pack[:slots, rank + 1], 0.0))
-    elements = count.astype(F32) * float(rows_all * cols)
-    totals = lax.psum(jnp.stack([squares, elements]), SEG)
-    clip = jnp.minimum(1.0, CLIP_RMS * lax.rsqrt(jnp.maximum(totals[0] / totals[1], SQUARE_FLOOR)))
-    left = jnp.where(keep, clip * math.sqrt(rows_all) * ortho, 0.0).astype(BF16)
-
-    line, left = lax.optimization_barrier((line, left))
     right = exchange(line, FAR_Z).astype(F32).sum(axis=0)
+    right, keep = lax.optimization_barrier((right, keep))
     half_right = whole_rows(right.astype(BF16))
     colsq = jnp.sum(jnp.square(half_right.astype(F32)), axis=1, keepdims=True)
     right_step = jnp.where(keep, right * (math.sqrt(cols) * lax.rsqrt(colsq + 1.0)), 0.0)

time: 217 us -> 210 us (0.968)
  blocking collectives: 127 us -> 143 us
  waiting for transfers between devices: 35 us -> 21.3 us
  Pallas kernels: 22.8 us -> 16.6 us
  matrix products: 4.31 us -> 8.35 us
  local copies, waits for them, and re-layouts: 6.35 us -> 3.15 us
  other arithmetic: 9.04 us -> 6.81 us
    all_to_all x6, blocking collectives: 116 us -> 133 us  [exchange(): return lax.all_to_all(blocks, axis, split_axis=0, concat_axis=0, tiled=True)]
    all_to_all x2, waiting for transfers between devices: 35 us -> 21.3 us  [exchange(): return lax.all_to_all(blocks, axis, split_axis=0, concat_axis=0, tiled=True)]
    pallas_call x2, Pallas kernels: 22.5 us -> 15.6 us  [the longest x1 14.1 us: factor(): pl.pallas_call(functools.partial(factor_kernel, near, math.sqrt(rows * de...]
    dot_general x0 -> x1, matrix products: none -> 4.04 us  [body(): proj = jnp.einsum('kij,kjr->kir', buffer, basis, preferred_element_type=F32)]
    unnamed x8 -> x4, local copies, waits for them, and re-layouts: 2.42 us -> 0.02 us
    convert_element_type x1 -> x0, other arithmetic: 2.32 us -> none  [body(): left = jnp.where(keep, clip * math.sqrt(rows_all) * ortho, 0.0).astype(BF16)]
  transfers between devices with their start and end apart: 2 -> 2, of which waited for: 2 -> 2; matrix products, arithmetic and copies ran while one was open for 4% -> 3% of each run, Pallas kernels for 0% -> 0%
where the time goes in v6:
time: 210 us; the launch traced here: 209 us
  blocking collectives  143 us (68%)
  waiting for transfers between devices  21.3 us (10%)
  Pallas kernels  16.6 us (8%)
  matrix products  8.35 us (4%)
  starting transfers between devices  8.25 us (4%)
  other arithmetic  6.81 us (3%)
  local copies, waits for them, and re-layouts  3.15 us (2%)
    all_to_all x6, blocking collectives, exchange(): return lax.all_to_all(blocks, axis, split_axis=0, concat_axis=0, tiled=True)  133 us
    all_to_all x2, waiting for transfers between devices, exchange(): return lax.all_to_all(blocks, axis, split_axis=0, concat_axis=0, tiled=True)  21.3 us
    pallas_call x1, Pallas kernels, factor(): pl.pallas_call(functools.partial(factor_kernel, near, math.sqrt(rows * de...  14.1 us
    psum x1, blocking collectives, body(): totals = lax.psum(jnp.stack([squares, elements]), SEG)  10.6 us
    all_to_all x2, starting transfers between devices, exchange(): return lax.all_to_all(blocks, axis, split_axis=0, concat_axis=0, tiled=True)  8.25 us
    dot_general x1, matrix products, body(): jnp.einsum('kir,kjr->kij', half_left, half_right, preferred_element_type=...  4.31 us
  transfers between devices with their start and end apart: 2, of which 2 were waited for; matrix products, arithmetic and copies ran while one was open for 3% of the time, Pallas kernels for 0%

profile of v6, /device:TPU:24, one launch (start us, length us, event | category | flops | bytes accessed | tf_op | source)
XLA Modules:
  0.0 209.2 jit_solution(10117239106979342034)
XLA Ops:
  0.6 0.9 broadcast_in_dim.48
  1.5 20.3 %all_to_all.40 = bf16[4,2,72,256]{3,2,1,0:T(8,128)(2,1)S(1)} all-to-all(bf16[4,2,72,256]{3,2,1,0:T(8,128)(2,1)S(1)} %broadcast_in_dim.48), channel_id=1, replica_groups=mesh['segment_0'=4,'segment_1'=2,'x'=4,'z_far'=4,'z_near'=2] {'z_far'}, dimensions={0} | all-to-all | bytes 589824 | tf_op jit(solution)/shard_map/all_to_all | solution.py:28
  21.8 1.6 broadcast_in_dim.49
  23.4 4.8 %all-to-all-start.1 = ((bf16[8,4,2,72,256]{4,3,2,1,0:T(8,128)(2,1)}), bf16[8,4,2,72,256]{4,3,2,1,0:T(8,128)(2,1)S(1)}, u32[]{:S(2)}, u32[]{:S(2)}) async-start(bf16[8,4,2,72,256]{4,3,2,1,0:T(8,128)(2,1)} %broadcast_in_dim.49), calls=%async_computation.1 | async-start | bytes 4718592 | tf_op jit(solution)/shard_map/all_to_all | solution.py:28
  28.8 4.0 %fusion = f32[2]{0:T(128)S(1)} fusion(bf16[2,576,2304]{2,1,0:T(8,128)(2,1)} %buffer_ref.1), kind=kLoop, calls=%fused_computation.2 | loop fusion | flops 7962622 | bytes 5308424 | tf_op jit(solution)/shard_map/reduce_sum | solution.py:213
  32.8 0.7 fusion.3
  33.5 0.8 pad_maximum_fusion
  34.3 10.6 %psum.7.total_ref = f32[2]{0:T(128)S(1)} all-reduce(f32[2]{0:T(128)S(1)} %pad_maximum_fusion), channel_id=1, replica_groups=mesh['segment_0'=4,'segment_1'=2,'x'=4,'z_far'=4,'z_near'=2] {'segment_0..., use_global_device_ids=true, to_apply=%region_2.3 | all-reduce | flops 2 | bytes 16 | tf_op jit(solution)/shard_map/psum | solution.py:216
  44.8 10.8 %all-to-all-done.1 = bf16[8,4,2,72,256]{4,3,2,1,0:T(8,128)(2,1)S(1)} async-done(((bf16[8,4,2,72,256]{4,3,2,1,0:T(8,128)(2,1)}), bf16[8,4,2,72,256]{4,3,2,1,0:T(8,128)(2,1)S(1)}, u32[]{:S(2)}, u32[]{:S(2)}) %all-to-all-start.1) | async-done | bytes 2359328 | tf_op jit(solution)/shard_map/all_to_all | solution.py:28
  55.7 0.2 copy.6
  55.9 4.0 %fusion.4.proj_ref = f32[2,576,256]{2,1,0:T(8,128)S(1)} fusion(bf16[2,576,2304]{2,1,0:T(8,128)(2,1)} %buffer_ref.1, bf16[2,2304,256]{2,1,0:T(8,128)(2,1)S(1)} %bitcast.29), kind=kOutput, calls=%fused_computation.13 | convolution fusion | flops 1358954496 | bytes 8847360 | tf_op jit(solution)/shard_map/kij,kjr->kir/dot_general | solution.py:217
  59.9 1.5 packed_grams.1
  61.4 18.7 %all_to_all.41 = f32[32,8,384]{2,1,0:T(8,128)S(1)} all-to-all(f32[32,8,384]{2,1,0:T(8,128)S(1)} %bitcast.21), channel_id=1, replica_groups=mesh['segment_0'=4,'segment_1'=2,'x'=4,'z_far'=4,'z_near'=2] {'x','z_far..., dimensions={0} | all-to-all | bytes 786432 | tf_op jit(solution)/shard_map/all_to_all | solution.py:28
  80.2 19.4 %all_to_all.42 = f32[32,8,384]{2,1,0:T(8,128)S(1)} all-to-all(f32[32,8,384]{2,1,0:T(8,128)S(1)} %broadcast_in_dim.50), channel_id=1, replica_groups=mesh['segment_0'=4,'segment_1'=2,'x'=4,'z_far'=4,'z_near'=2] {'x','z_far..., dimensions={0} | all-to-all | bytes 786432 | tf_op jit(solution)/shard_map/all_to_all | solution.py:28
  99.6 14.1 %factor.1 = (bf16[2,576,256]{2,1,0:T(8,128)(2,1)}, bf16[2,576,256]{2,1,0:T(8,128)(2,1)S(1)}, bf16[8,4,2,72,256]{4,3,2,1,0:T(8,128)(2,1)S(1)}) custom-call(s32[1]{0:T(128)} %copy.8.count_ref, f32[256,384]{1,0:T(8,128)S(1)} %bitcast.22, f32[2,576,256]{2,1,0:T(8,128)S(1)} %fusion.4.proj_ref, bf16[2,576,2304]{2,1,0:T(8,128)(2,1)} %buffer_ref.1), custom_call_target="tpu_custom_call" | custom-call | tf_op jit(solution)/shard_map/factor/pallas_call | solution.py:165
  113.7 33.0 %all_to_all.43.blocks_ref = bf16[8,4,2,72,256]{4,3,2,1,0:T(8,128)(2,1)S(1)} all-to-all(bf16[8,4,2,72,256]{4,3,2,1,0:T(8,128)(2,1)S(1)} %get-tuple-element.8), channel_id=1, replica_groups=mesh['segment_0'=4,'segment_1'=2,'x'=4,'z_far'=4,'z_near'=2] {'x','z_near'}, dimensions={0} | all-to-all | bytes 4718592 | tf_op jit(solution)/shard_map/all_to_all | solution.py:28
  146.6 1.0 added.1
  147.6 3.5 %all-to-all-start.5 = ((bf16[4,2,72,256]{3,2,1,0:T(8,128)(2,1)}), bf16[4,2,72,256]{3,2,1,0:T(8,128)(2,1)S(1)}, u32[]{:S(2)}, u32[]{:S(2)}) async-start(bf16[4,2,72,256]{3,2,1,0:T(8,128)(2,1)} %added.1), calls=%async_computation.5 | async-start | bytes 589824 | tf_op jit(solution)/shard_map/all_to_all | solution.py:28
  151.1 10.4 %all-to-all-done.5 = bf16[4,2,72,256]{3,2,1,0:T(8,128)(2,1)S(1)} async-done(((bf16[4,2,72,256]{3,2,1,0:T(8,128)(2,1)}), bf16[4,2,72,256]{3,2,1,0:T(8,128)(2,1)S(1)}, u32[]{:S(2)}, u32[]{:S(2)}) %all-to-all-start.5) | async-done | bytes 294944 | tf_op jit(solution)/shard_map/all_to_all | solution.py:28
  161.6 0.0 slice-start
  161.6 13.0 %all_to_all.44 = bf16[4,2,72,256]{3,2,1,0:T(8,128)(2,1)S(1)} all-to-all(bf16[4,2,72,256]{3,2,1,0:T(8,128)(2,1)S(1)} %broadcast_in_dim.53), channel_id=1, replica_groups=mesh['segment_0'=4,'segment_1'=2,'x'=4,'z_far'=4,'z_near'=2] {'z_far'}, dimensions={0} | all-to-all | bytes 589824 | tf_op jit(solution)/shard_map/all_to_all | solution.py:28
  174.7 0.2 broadcast_in_dim.54
  174.9 0.0 slice-start.1
  174.9 28.5 %all_to_all.45 = bf16[8,4,2,72,256]{4,3,2,1,0:T(8,128)(2,1)S(1)} all-to-all(bf16[8,4,2,72,256]{4,3,2,1,0:T(8,128)(2,1)S(1)} %broadcast_in_dim.54), channel_id=1, replica_groups=mesh['segment_0'=4,'segment_1'=2,'x'=4,'z_far'=4,'z_near'=2] {'x','z_near'}, dimensions={0} | all-to-all | bytes 4718592 | tf_op jit(solution)/shard_map/all_to_all | solution.py:28
  203.4 0.5 multiply_reduce_fusion
  203.9 0.2 copy.7
  204.2 0.7 multiply_select_fusion
  204.9 0.0 slice-done
  204.9 0.0 slice-done.1
  204.9 4.3 %fusion.2 = bf16[2,576,2304]{2,1,0:T(8,128)(2,1)} fusion(bf16[2,576,2304]{2,1,0:T(8,128)(2,1)S(1)} %bitcast.24, bf16[2,576,256]{2,1,0:T(8,128)(2,1)S(1)} %get-tuple-element.10, bf16[2,2304,256]{2,1,0:T(8,128)(2,1)S(1)} %bitcast.28, pred[2]{0:T(512)(128)(4,1)S(1)} %bitcast.31), kind=kOutput, calls=%fused_computation.4 | convolution fusion | flops 1372225536 | bytes 13565954 | tf_op jit(solution)/shard_map/kir,kjr->kij/dot_general | solution.py:230
  (8 shorter events, 0.2 us)
Async XLA Ops:
  23.4 32.3 %all-to-all-start.1 = ((bf16[8,4,2,72,256]{4,3,2,1,0:T(8,128)(2,1)}), bf16[8,4,2,72,256]{4,3,2,1,0:T(8,128)(2,1)S(1)}, u32[]{:S(2)}, u32[]{:S(2)}) async-start(bf16[8,4,2,72,256]{4,3,2,1,0:T(8,128)(2,1)} %broadcast_in_dim.49), calls=%async_computation.1 | async-start | bytes 4718592 | tf_op jit(solution)/shard_map/all_to_all | solution.py:28
  147.6 13.9 %all-to-all-start.5 = ((bf16[4,2,72,256]{3,2,1,0:T(8,128)(2,1)}), bf16[4,2,72,256]{3,2,1,0:T(8,128)(2,1)S(1)}, u32[]{:S(2)}, u32[]{:S(2)}) async-start(bf16[4,2,72,256]{3,2,1,0:T(8,128)(2,1)} %added.1), calls=%async_computation.5 | async-start | bytes 589824 | tf_op jit(solution)/shard_map/all_to_all | solution.py:28
  161.6 43.3 %slice-start = ((s8[5308416]{0:T(1024)(128)(4,1)}), s8[4194304]{0:T(1024)(128)(4,1)S(1)}, s32[]{:S(2)}) async-start(s8[5308416]{0:T(1024)(128)(4,1)} %bitcast.23), calls=%async_computation.8 | async-start | bytes 8388608
  174.9 30.1 %slice-start.1 = ((s8[5308416]{0:T(1024)(128)(4,1)}), s8[1114112]{0:T(1024)(128)(4,1)S(1)}, s32[]{:S(2)}) async-start(s8[5308416]{0:T(1024)(128)(4,1)} %bitcast.23), calls=%async_computation.9 | async-start | bytes 2228224

commit v7 on v6

--- a/solution.py
+++ b/solution.py
@@ -32,9 +32,9 @@
     return exchange(jnp.broadcast_to(value, (lax.axis_size(axis), *value.shape)), axis)
 
 
-def whole_rows(shard):
-    slots, rows, rank = shard.shape
-    plane = spread(spread(shard, FAR_Z), PLANE)
+def whole_rows(line):
+    slots, rows, rank = line.shape[1:]
+    plane = spread(line, PLANE)
     plane = plane.reshape(lax.axis_size(X), lax.axis_size(NEAR_Z), -1, slots, rows, rank)
     return plane.transpose(3, 0, 2, 1, 4, 5).reshape(slots, -1, rank)
 
@@ -209,11 +209,12 @@
     used = jnp.arange(slots, dtype=jnp.int32) < count
     keep = used[:, None, None]
 
-    basis = whole_rows(right_basis)
     squares = jnp.sum(jnp.square(buffer.astype(F32)), axis=(1, 2))
     squares = jnp.sum(jnp.where(used, squares, 0.0))
     elements = count.astype(F32) * float(rows_dev * cols)
     totals = lax.psum(jnp.stack([squares, elements]), SEG)
+    line, totals, keep = lax.optimization_barrier((spread(right_basis, FAR_Z), totals, keep))
+    basis = whole_rows(line)
     proj = jnp.einsum("kij,kjr->kir", buffer, basis, preferred_element_type=F32)
     pack = packed_grams(proj, totals)
     part = exchange(pack.reshape(devices, -1, pack.shape[-1]), SHARD).sum(axis=0)
@@ -222,8 +223,7 @@
     left, half_left, blocks = factor(layer_count, pack, proj, buffer, *sizes)
     line = added(exchange(blocks, PLANE))
     right = exchange(line, FAR_Z).astype(F32).sum(axis=0)
-    right, keep = lax.optimization_barrier((right, keep))
-    half_right = whole_rows(right.astype(BF16))
+    half_right = whole_rows(spread(right.astype(BF16), FAR_Z))
     colsq = jnp.sum(jnp.square(half_right.astype(F32)), axis=1, keepdims=True)
     right_step = jnp.where(keep, right * (math.sqrt(cols) * lax.rsqrt(colsq + 1.0)), 0.0)
 

time: 210 us -> 218 us (1.038)
  blocking collectives: 143 us -> 176 us
  waiting for transfers between devices: 21.3 us -> 0.01 us
  matrix products: 8.35 us -> 5.85 us
    all_to_all x6 -> x7, blocking collectives: 133 us -> 166 us  [exchange(): return lax.all_to_all(blocks, axis, split_axis=0, concat_axis=0, tiled=True)]
    all_to_all x2 -> x1, waiting for transfers between devices: 21.3 us -> 0.01 us  [exchange(): return lax.all_to_all(blocks, axis, split_axis=0, concat_axis=0, tiled=True)]
    dot_general x1, matrix products: 4.04 us -> 1.53 us  [body(): proj = jnp.einsum('kij,kjr->kir', buffer, basis, preferred_element_type=F32)]
    all_to_all x2 -> x1, starting transfers between devices: 8.25 us -> 8.46 us  [exchange(): return lax.all_to_all(blocks, axis, split_axis=0, concat_axis=0, tiled=True)]
  transfers between devices with their start and end apart: 2 -> 1, of which waited for: 2 -> 0; matrix products, arithmetic and copies ran while one was open for 3% -> 2% of each run, Pallas kernels for 0% -> 0%
where the time goes in v7:
time: 218 us; the launch traced here: 217 us
  blocking collectives  176 us (81%)
  Pallas kernels  15.9 us (7%)
  starting transfers between devices  8.46 us (4%)
  other arithmetic  6.81 us (3%)
  matrix products  5.85 us (3%)
  local copies, waits for them, and re-layouts  2.46 us (1%)
    all_to_all x7, blocking collectives, exchange(): return lax.all_to_all(blocks, axis, split_axis=0, concat_axis=0, tiled=True)  166 us
    pallas_call x1, Pallas kernels, factor(): pl.pallas_call(functools.partial(factor_kernel, near, math.sqrt(rows * de...  14.1 us
    psum x1, blocking collectives, body(): totals = lax.psum(jnp.stack([squares, elements]), SEG)  10.4 us
    all_to_all x1, starting transfers between devices, exchange(): return lax.all_to_all(blocks, axis, split_axis=0, concat_axis=0, tiled=True)  8.46 us
  transfers between devices with their start and end apart: 1, of which 0 were waited for; matrix products, arithmetic and copies ran while one was open for 2% of the time, Pallas kernels for 0%

profile of v7, /device:TPU:24, one launch (start us, length us, event | category | flops | bytes accessed | tf_op | source)
XLA Modules:
  0.0 217.1 jit_solution(9182783827646697880)
XLA Ops:
  0.6 1.6 broadcast_in_dim.47
  2.2 8.5 %all-to-all-start = ((bf16[4,2,72,256]{3,2,1,0:T(8,128)(2,1)}), bf16[4,2,72,256]{3,2,1,0:T(8,128)(2,1)S(1)}, u32[]{:S(2)}, u32[]{:S(2)}) async-start(bf16[4,2,72,256]{3,2,1,0:T(8,128)(2,1)} %broadcast_in_dim.47), calls=%async_computation | async-start | bytes 589824 | tf_op jit(solution)/shard_map/all_to_all | solution.py:28
  10.7 4.0 %fusion = f32[2]{0:T(128)S(1)} fusion(bf16[2,576,2304]{2,1,0:T(8,128)(2,1)} %buffer_ref.1), kind=kLoop, calls=%fused_computation.2 | loop fusion | flops 7962622 | bytes 5308424 | tf_op jit(solution)/shard_map/reduce_sum | solution.py:212
  15.3 0.7 fusion.3
  16.0 0.8 pad_maximum_fusion
  16.8 10.4 %psum.7.total_ref = f32[2]{0:T(128)S(1)} all-reduce(f32[2]{0:T(128)S(1)} %pad_maximum_fusion), channel_id=1, replica_groups=mesh['segment_0'=4,'segment_1'=2,'x'=4,'z_far'=4,'z_near'=2] {'segment_0..., use_global_device_ids=true, to_apply=%region_2.3 | all-reduce | flops 2 | bytes 16 | tf_op jit(solution)/shard_map/psum | solution.py:215
  27.2 0.0 all-to-all-done
  27.2 0.0 slice-start
  27.2 0.2 broadcast_in_dim.51
  27.4 0.0 slice-start.1
  27.4 35.7 %all_to_all.40 = bf16[8,4,2,72,256]{4,3,2,1,0:T(8,128)(2,1)S(1)} all-to-all(bf16[8,4,2,72,256]{4,3,2,1,0:T(8,128)(2,1)S(1)} %broadcast_in_dim.51), channel_id=1, replica_groups=mesh['segment_0'=4,'segment_1'=2,'x'=4,'z_far'=4,'z_near'=2] {'x','z_near'}, dimensions={0} | all-to-all | bytes 4718592 | tf_op jit(solution)/shard_map/all_to_all | solution.py:28
  63.1 0.2 copy.6
  63.3 0.0 slice-done
  63.4 0.0 slice-done.1
  63.4 1.5 convolution_bitcast_fusion.proj_ref
  64.9 1.5 packed_grams.1
  66.4 22.2 %all_to_all.41 = f32[32,8,384]{2,1,0:T(8,128)S(1)} all-to-all(f32[32,8,384]{2,1,0:T(8,128)S(1)} %bitcast.23), channel_id=1, replica_groups=mesh['segment_0'=4,'segment_1'=2,'x'=4,'z_far'=4,'z_near'=2] {'x','z_far..., dimensions={0} | all-to-all | bytes 786432 | tf_op jit(solution)/shard_map/all_to_all | solution.py:28
  88.7 19.4 %all_to_all.42 = f32[32,8,384]{2,1,0:T(8,128)S(1)} all-to-all(f32[32,8,384]{2,1,0:T(8,128)S(1)} %broadcast_in_dim.52), channel_id=1, replica_groups=mesh['segment_0'=4,'segment_1'=2,'x'=4,'z_far'=4,'z_near'=2] {'x','z_far..., dimensions={0} | all-to-all | bytes 786432 | tf_op jit(solution)/shard_map/all_to_all | solution.py:28
  108.1 14.1 %factor.1 = (bf16[2,576,256]{2,1,0:T(8,128)(2,1)}, bf16[2,576,256]{2,1,0:T(8,128)(2,1)S(1)}, bf16[8,4,2,72,256]{4,3,2,1,0:T(8,128)(2,1)S(1)}) custom-call(s32[1]{0:T(128)} %copy.8.count_ref, f32[256,384]{1,0:T(8,128)S(1)} %bitcast.24, f32[2,576,256]{2,1,0:T(8,128)S(1)} %convolution_bitcast_fusion.proj_ref, bf16[2,576,2304]{2,1,0:T(8,128)(2,1)} %buffer_ref.1), custom_call_target="tpu_custom_call" | custom-call | tf_op jit(solution)/shard_map/factor/pallas_call | solution.py:165
  122.2 32.9 %all_to_all.43.blocks_ref = bf16[8,4,2,72,256]{4,3,2,1,0:T(8,128)(2,1)S(1)} all-to-all(bf16[8,4,2,72,256]{4,3,2,1,0:T(8,128)(2,1)S(1)} %get-tuple-element.13), channel_id=1, replica_groups=mesh['segment_0'=4,'segment_1'=2,'x'=4,'z_far'=4,'z_near'=2] {'x','z_near'}, dimensions={0} | all-to-all | bytes 4718592 | tf_op jit(solution)/shard_map/all_to_all | solution.py:28
  155.2 0.3 added.1
  155.5 13.3 %all_to_all.44 = bf16[4,2,72,256]{3,2,1,0:T(8,128)(2,1)S(1)} all-to-all(bf16[4,2,72,256]{3,2,1,0:T(8,128)(2,1)S(1)} %added.1), channel_id=1, replica_groups=mesh['segment_0'=4,'segment_1'=2,'x'=4,'z_far'=4,'z_near'=2] {'z_far'}, dimensions={0} | all-to-all | bytes 589824 | tf_op jit(solution)/shard_map/all_to_all | solution.py:28
  168.8 0.0 slice-start.2
  168.8 13.5 %all_to_all.45 = bf16[4,2,72,256]{3,2,1,0:T(8,128)(2,1)S(1)} all-to-all(bf16[4,2,72,256]{3,2,1,0:T(8,128)(2,1)S(1)} %broadcast_in_dim.53), channel_id=1, replica_groups=mesh['segment_0'=4,'segment_1'=2,'x'=4,'z_far'=4,'z_near'=2] {'z_far'}, dimensions={0} | all-to-all | bytes 589824 | tf_op jit(solution)/shard_map/all_to_all | solution.py:28
  182.3 0.2 broadcast_in_dim.54
  182.5 0.0 slice-start.3
  182.5 28.7 %all_to_all.46 = bf16[8,4,2,72,256]{4,3,2,1,0:T(8,128)(2,1)S(1)} all-to-all(bf16[8,4,2,72,256]{4,3,2,1,0:T(8,128)(2,1)S(1)} %broadcast_in_dim.54), channel_id=1, replica_groups=mesh['segment_0'=4,'segment_1'=2,'x'=4,'z_far'=4,'z_near'=2] {'x','z_near'}, dimensions={0} | all-to-all | bytes 4718592 | tf_op jit(solution)/shard_map/all_to_all | solution.py:28
  211.2 0.5 multiply_reduce_fusion
  211.8 0.2 copy.7
  212.0 0.7 multiply_select_fusion
  212.8 0.0 slice-done.2
  212.8 0.0 slice-done.3
  212.8 4.3 %fusion.2 = bf16[2,576,2304]{2,1,0:T(8,128)(2,1)} fusion(bf16[2,576,2304]{2,1,0:T(8,128)(2,1)S(1)} %bitcast.28, bf16[2,576,256]{2,1,0:T(8,128)(2,1)S(1)} %get-tuple-element.12, bf16[2,2304,256]{2,1,0:T(8,128)(2,1)S(1)} %bitcast.32, pred[2]{0:T(512)(128)(4,1)S(1)} %bitcast.35), kind=kOutput, calls=%fused_computation.4 | convolution fusion | flops 1372225536 | bytes 13565954 | tf_op jit(solution)/shard_map/kir,kjr->kij/dot_general | solution.py:230
  (9 shorter events, 0.2 us)
Async XLA Ops:
  2.2 25.0 %all-to-all-start = ((bf16[4,2,72,256]{3,2,1,0:T(8,128)(2,1)}), bf16[4,2,72,256]{3,2,1,0:T(8,128)(2,1)S(1)}, u32[]{:S(2)}, u32[]{:S(2)}) async-start(bf16[4,2,72,256]{3,2,1,0:T(8,128)(2,1)} %broadcast_in_dim.47), calls=%async_computation | async-start | bytes 589824 | tf_op jit(solution)/shard_map/all_to_all | solution.py:28
  27.2 36.1 %slice-start = ((s8[5308416]{0:T(1024)(128)(4,1)}), s8[4194304]{0:T(1024)(128)(4,1)S(1)}, s32[]{:S(2)}) async-start(s8[5308416]{0:T(1024)(128)(4,1)} %bitcast.25), calls=%async_computation.8 | async-start | bytes 8388608
  27.4 35.9 %slice-start.1 = ((s8[5308416]{0:T(1024)(128)(4,1)}), s8[1114112]{0:T(1024)(128)(4,1)S(1)}, s32[]{:S(2)}) async-start(s8[5308416]{0:T(1024)(128)(4,1)} %bitcast.25), calls=%async_computation.9 | async-start | bytes 2228224
  168.8 44.0 %slice-start.2 = ((s8[5308416]{0:T(1024)(128)(4,1)}), s8[4194304]{0:T(1024)(128)(4,1)S(1)}, s32[]{:S(2)}) async-start(s8[5308416]{0:T(1024)(128)(4,1)} %bitcast.27), calls=%async_computation.10 | async-start | bytes 8388608
  182.5 30.2 %slice-start.3 = ((s8[5308416]{0:T(1024)(128)(4,1)}), s8[1114112]{0:T(1024)(128)(4,1)S(1)}, s32[]{:S(2)}) async-start(s8[5308416]{0:T(1024)(128)(4,1)} %bitcast.27), calls=%async_computation.11 | async-start | bytes 2228224
